TPU v7x, 32 devices: a whole 2x2x4 slice. The times are simulated.
32 devices in a mesh: rep: 4 (over x, y), dp: 8 (over z, core).
Axes of the slice: x: 2, y: 2, z: 4, core: 2. Of those that a mesh axis runs over, the one named last changes fastest.
Arguments:
- x: bfloat16 [32, 2048, 1024], P(('rep', 'dp')), parts along dimension 0
- dy: bfloat16 [32, 2048, 1024], P(('rep', 'dp')), parts along dimension 0
- w_gate: bfloat16 [2, 1024, 3200], replicated
- w_up: bfloat16 [2, 1024, 3200], replicated
- w_down: bfloat16 [2, 3200, 1024], replicated
- m_w_gate: float32 [2, 1024, 3200], replicated
- m_w_up: float32 [2, 1024, 3200], replicated
- m_w_down: float32 [2, 3200, 1024], replicated
- v_w_gate: float32 [2, 1024, 3200], replicated
- v_w_up: float32 [2, 1024, 3200], replicated
- v_w_down: float32 [2, 3200, 1024], replicated
Outputs:
- output 1: bfloat16 [8, 1024, 3200], P('rep'), parts along dimension 0
- output 2: bfloat16 [8, 1024, 3200], P('rep'), parts along dimension 0
- output 3: bfloat16 [8, 3200, 1024], P('rep'), parts along dimension 0
- output 4: float32 [8, 1024, 3200], P('rep'), parts along dimension 0
- output 5: float32 [8, 1024, 3200], P('rep'), parts along dimension 0
- output 6: float32 [8, 3200, 1024], P('rep'), parts along dimension 0
- output 7: float32 [8, 1024, 3200], P('rep'), parts along dimension 0
- output 8: float32 [8, 1024, 3200], P('rep'), parts along dimension 0
- output 9: float32 [8, 3200, 1024], P('rep'), parts along dimension 0
There are 4 independent parts. A program takes and returns all parts, laid end to end along the dimension named above; an argument that names none is the same for every part.
All inputs are finite; a program needn't handle non-finite values.
Results may differ from a plain program's by a relative error of at most 0.022.
Values are sent between devices in bfloat16 or wider.
A program may use at most 2.75 GiB of HBM per device.

v0:
```python
import jax
import jax.numpy as jnp
from jax import lax
from jax.sharding import PartitionSpec as P

NAMES = ("w_gate", "w_up", "w_down")


def matmul(a, w):
    return jnp.dot(a, w, preferred_element_type=jnp.float32).astype(jnp.bfloat16)


def normed(h):
    wide = h.astype(jnp.float32)
    scale = lax.rsqrt(jnp.mean(wide**2, -1, keepdims=True) + 1e-6)
    return (wide * scale).astype(jnp.bfloat16)


def layer(h, w):
    a = normed(h)
    gate = jnp.dot(a, w["w_gate"], preferred_element_type=jnp.float32)
    up = jnp.dot(a, w["w_up"], preferred_element_type=jnp.float32)
    return h + matmul((jax.nn.silu(gate) * up).astype(jnp.bfloat16), w["w_down"])


def adamw(w, m, v, g):
    m = 0.9 * m + 0.1 * g
    v = 0.95 * v + 0.05 * g * g
    step = m * lax.rsqrt(v + 1e-8) + 0.1 * w
    return (w - 0.02 * step).astype(jnp.bfloat16), m, v


def solution(mesh):
    def step(x, dy, *arrays):
        weights, m, v = (arrays[i : i + 3] for i in (0, 3, 6))
        layers = weights[0].shape[0]
        h, kept = x[0], []
        for number in range(layers):
            kept.append(h)
            h = layer(h, {name: w[number] for name, w in zip(NAMES, weights, strict=True)})
        by_h, summed = dy[0], [None] * layers
        for number in reversed(range(layers)):
            _, back = jax.vjp(lambda w, h: layer(h, w), {name: w[number] for name, w in zip(NAMES, weights, strict=True)}, kept[number])
            by_w, by_h = back(by_h)
            summed[number] = [lax.psum(by_w[name], "dp") for name in NAMES]
        gradients = [jnp.stack([summed[number][i] for number in range(layers)]).astype(jnp.float32) for i in range(3)]
        new = [adamw(w.astype(jnp.float32), m, v, g) for w, m, v, g in zip(weights, m, v, gradients, strict=True)]
        return tuple(one[which] for which in range(3) for one in new)

    return jax.shard_map(
        step,
        mesh=mesh,
        in_specs=(P(("rep", "dp"), None, None),) * 2 + (P(None, None, None),) * 9,
        out_specs=(P("rep", None, None),) * 9,
        check_vma=False,
    )
```

profile of v0, /device:TPU:27, one launch (start us, length us, event | category | flops | bytes accessed | tf_op | source)
XLA Modules:
  0.0 1305.8 jit_solution(13645570414355317417)
XLA Ops:
  7.2 0.0 all-reduce.3.cloned.1.call-start
  7.2 6.5 copy.20
  13.7 3.1 fusion.30
  16.8 6.5 copy.21
  23.3 20.9 %convolution_convert_fusion.1 = bf16[2048,3200]{1,0:T(8,128)(2,1)} fusion(bf16[2,3200,1024]{2,1,0:T(8,128)(2,1)} %param.15, bf16[1,2048,1024]{2,1,0:T(8,128)(2,1)} %param.12), kind=kOutput, calls=%fused_computation.50 | convolution fusion | flops 13428326400 | bytes 23855104 | tf_op jit(solution)/shard_map/transpose(jvp())/dot_general | solution.py:10
  44.2 20.9 %fusion.56 = f32[2048,3200]{1,0:T(8,128)} fusion(bf16[2,1024,3200]{2,1,0:T(8,128)(2,1)} %param.13, bf16[1,2048,1024]{2,1,0:T(8,128)(2,1)S(1)} %copy-done.3, f32[2048]{0:T(1024)S(1)} %add_rsqrt_fusion), kind=kOutput, calls=%fused_computation.90 | convolution fusion | flops 13428064256 | bytes 36970496 | tf_op jit(solution)/shard_map/dot_general | solution.py:21
  65.1 32.4 %multiply_convert_fusion.1 = (bf16[2048,3200]{1,0:T(8,128)(2,1)}, f32[2048,3200]{1,0:T(8,128)}) fusion(f32[2048,3200]{1,0:T(8,128)} %fusion.56, bf16[2,1024,3200]{2,1,0:T(8,128)(2,1)} %param.14, bf16[1,2048,1024]{2,1,0:T(8,128)(2,1)} %param.11, f32[2048]{0:T(1024)S(1)} %add_rsqrt_fusion), kind=kOutput, calls=%fused_computation.44 | convolution fusion | flops 13467385856 | bytes 76292096 | tf_op jit(solution)/shard_map/dot_general | solution.py:22
  97.6 21.9 %fusion.34 = (f32[2048]{0:T(1024)S(1)}, bf16[2048,1024]{0,1:T(8,128)(2,1)}) fusion(bf16[2048,3200]{1,0:T(8,128)(2,1)} %get-tuple-element.24, bf16[2,3200,1024]{2,1,0:T(8,128)(2,1)} %param.15, bf16[1,2048,1024]{1,2,0:T(8,128)(2,1)} %copy.20), kind=kOutput, calls=%fused_computation.67 | convolution fusion | flops 13432256512 | bytes 28057600 | tf_op jit(solution)/shard_map/dot_general | solution.py:10
  119.4 23.3 %fusion.43 = f32[2048,3200]{1,0:T(8,128)} fusion(bf16[2,1024,3200]{2,1,0:T(8,128)(2,1)} %param.14, bf16[2048,1024]{0,1:T(8,128)(2,1)} %get-tuple-element.27, f32[2048]{0:T(1024)S(1)} %fusion.92), kind=kOutput, calls=%fused_computation.77 | convolution fusion | flops 13428064256 | bytes 36970496 | tf_op jit(solution)/shard_map/jvp()/dot_general | solution.py:22
  142.8 38.9 %fusion.14 = (bf16[2048,3200]{1,0:T(8,128)(2,1)}, f32[2048,3200]{1,0:T(8,128)}) fusion(f32[2048,3200]{1,0:T(8,128)} %fusion.43, bf16[2048,3200]{1,0:T(8,128)(2,1)} %convolution_convert_fusion.1, bf16[2,1024,3200]{2,1,0:T(8,128)(2,1)} %param.13, bf16[2048,1024]{0,1:T(8,128)(2,1)} %get-tuple-element.27, f32[2048]{0:T(1024)S(1)} %fusion.92), kind=kOutput, calls=%fused_computation.32 | convolution fusion | flops 13506707456 | bytes 89399296 | tf_op jit(solution)/shard_map/jvp()/dot_general | solution.py:21
  181.7 22.6 %fusion.27 = bf16[2048,1024]{0,1:T(8,128)(2,1)} fusion(bf16[2048,3200]{1,0:T(8,128)(2,1)} %convolution_convert_fusion.1, bf16[2,1024,3200]{2,1,0:T(8,128)(2,1)} %param.14, f32[2048,3200]{1,0:T(8,128)} %get-tuple-element.29), kind=kOutput, calls=%fused_computation.48 | convolution fusion | flops 13461094400 | bytes 50069504 | tf_op jit(solution)/shard_map/transpose(jvp())/dot_general | solution.py:22
  204.3 24.2 %fusion.64 = bf16[1,1024,3200]{2,1,0:T(8,128)(2,1)} fusion(bf16[2048,3200]{1,0:T(8,128)(2,1)} %convolution_convert_fusion.1, bf16[2048,1024]{0,1:T(8,128)(2,1)S(1)} %copy-done.2, f32[2048]{0:T(1024)S(1)} %fusion.92, f32[2048,3200]{1,0:T(8,128)} %get-tuple-element.29), kind=kOutput, calls=%fused_computation.98 | convolution fusion | flops 13470662656 | bytes 50077696 | tf_op jit(solution)/shard_map/transpose(jvp())/dot_general | solution.py:22
  228.5 25.9 %fusion.65 = bf16[1,3200,1024]{2,1,0:T(8,128)(2,1)} fusion(f32[2048,3200]{1,0:T(8,128)} %fusion.43, bf16[1,2048,1024]{2,1,0:T(8,128)(2,1)} %param.12, f32[2048,3200]{1,0:T(8,128)} %get-tuple-element.29), kind=kOutput, calls=%fused_computation.99 | convolution fusion | flops 13464371200 | bytes 63176704 | tf_op jit(solution)/shard_map/transpose(jvp())/dot_general | solution.py:10
  254.4 21.2 %fusion.61 = bf16[1,1024,3200]{2,1,0:T(8,128)(2,1)} fusion(bf16[2048,3200]{1,0:T(8,128)(2,1)} %get-tuple-element.28, bf16[2048,1024]{0,1:T(8,128)(2,1)} %get-tuple-element.27, f32[2048]{0:T(1024)S(1)} %fusion.92), kind=kOutput, calls=%fused_computation.95 | convolution fusion | flops 13428064256 | bytes 23863296 | tf_op jit(solution)/shard_map/transpose(jvp())/dot_general | solution.py:21
  275.6 22.8 %fusion.36 = (f32[2048]{0:T(1024)S(1)}, bf16[2048,1024]{0,1:T(8,128)(2,1)}) fusion(bf16[2048,1024]{0,1:T(8,128)(2,1)} %get-tuple-element.27, bf16[2048,1024]{0,1:T(8,128)(2,1)} %fusion.27, bf16[2048,3200]{1,0:T(8,128)(2,1)} %get-tuple-element.28, bf16[2,1024,3200]{2,1,0:T(8,128)(2,1)} %param.13), kind=kOutput, calls=%fused_computation.69 | convolution fusion | flops 13432256512 | bytes 32251904 | tf_op jit(solution)/shard_map/transpose(jvp())/dot_general | solution.py:21
  298.4 6.6 fusion.77
  305.1 21.1 %convolution_convert_fusion = bf16[2048,3200]{1,0:T(8,128)(2,1)} fusion(bf16[2048,1024]{0,1:T(8,128)(2,1)} %fusion.77, bf16[2,3200,1024]{2,1,0:T(8,128)(2,1)} %param.15), kind=kOutput, calls=%fused_computation.49 | convolution fusion | flops 13428326400 | bytes 23855104 | tf_op jit(solution)/shard_map/transpose(jvp())/dot_general | solution.py:10
  326.2 21.2 %fusion.62 = bf16[1,3200,1024]{2,1,0:T(8,128)(2,1)} fusion(bf16[2048,3200]{1,0:T(8,128)(2,1)} %get-tuple-element.24, bf16[2048,1024]{0,1:T(8,128)(2,1)} %fusion.77), kind=kOutput, calls=%fused_computation.96 | convolution fusion | flops 13425049600 | bytes 23855104 | tf_op jit(solution)/shard_map/transpose(jvp())/dot_general | solution.py:10
  347.4 24.2 %fusion.63 = bf16[1,1024,3200]{2,1,0:T(8,128)(2,1)} fusion(bf16[2048,3200]{1,0:T(8,128)(2,1)} %convolution_convert_fusion, f32[2048,3200]{1,0:T(8,128)} %fusion.56, bf16[1,2048,1024]{1,2,0:T(8,128)(2,1)S(1)} %copy-done.1, f32[2048]{0:T(1024)S(1)} %copy-done.7), kind=kOutput, calls=%fused_computation.97 | convolution fusion | flops 13470662656 | bytes 50077696 | tf_op jit(solution)/shard_map/transpose(jvp())/dot_general | solution.py:22
  371.5 29.6 %fusion.66 = bf16[1,1024,3200]{2,1,0:T(8,128)(2,1)} fusion(f32[2048,3200]{1,0:T(8,128)} %fusion.56, f32[2048,3200]{1,0:T(8,128)} %get-tuple-element.25, bf16[2048,3200]{1,0:T(8,128)(2,1)} %convolution_convert_fusion, bf16[1,2048,1024]{1,2,0:T(8,128)(2,1)S(1)} %copy-done.1, f32[2048]{0:T(1024)S(1)} %copy-done.7), kind=kOutput, calls=%fused_computation.100 | convolution fusion | flops 13503430656 | bytes 76292096 | tf_op jit(solution)/shard_map/transpose(jvp())/dot_general | solution.py:21
  401.2 0.0 all-reduce.3.cloned.1.call-update
  401.2 756.2 %all-reduce.3.cloned.1.call-done = (bf16[1,1024,3200]{2,1,0:T(8,128)(2,1)}, bf16[1,1024,3200]{2,1,0:T(8,128)(2,1)}, bf16[1,1024,3200]{2,1,0:T(8,128)(2,1)}, bf16...) async-done(((bf16[1,1024,3200]{2,1,0:T(8,128)(2,1)}, bf16[1,1024,3200]{2,1,0:T(8,128)(2,1)}, ...) | async-done | bytes 39321616 | tf_op jit(solution)/shard_map/psum | solution.py:45
  1157.4 49.7 %fusion.11 = (bf16[2,3200,1024]{2,1,0:T(8,128)(2,1)}, f32[2,3200,1024]{2,1,0:T(8,128)}, f32[2,3200,1024]{2,1,0:T(8,128)}) fusion(bf16[2,3200,1024]{2,1,0:T(8,128)(2,1)} %param.15, bf16[1,3200,1024]{2,1,0:T(8,128)(2,1)} %get-tuple-element.13, bf16[1,3200,1024]{2,1,0:T(8,128)(2,1)} %get-tuple-element.14, f32[2,3200,1024]{2,1,0:T(8,128)} %param.21, ...), kind=kLoop, calls=%fused_computation.29 | loop fusion | flops 124518400 | bytes 144179200 | tf_op jit(solution)/shard_map/convert_element_type | solution.py:30
  1207.1 91.6 %fusion.2 = (bf16[2,1024,3200]{2,1,0:T(8,128)(2,1)}, f32[2,1024,3200]{2,1,0:T(8,128)}, f32[2,1024,3200]{2,1,0:T(8,128)}, bf16[2,1024,3200]{2,1,0:T(8,128)(2,1)},...) fusion(bf16[2,1024,3200]{2,1,0:T(8,128)(2,1)} %param.13, bf16[1,1024,3200]{2,1,0:T(8,128)(2,1)} %get-tuple-element.9, ...), kind=kLoop, calls=%fused_computation.20 | loop fusion | flops 249036800 | bytes 288358400 | tf_op jit(solution)/shard_map/convert_element_type | solution.py:30
  (19 shorter events, 0.1 us)
Async XLA Ops:
  7.2 1150.2 %all-reduce.3.cloned.1.call-start = ((), (), s32[]{:S(2)}) async-start(), calls=%async_computation | async-start | bytes 78643200 | tf_op jit(solution)/shard_map/psum | solution.py:45
  16.8 48.3 %copy-start.6 = (f32[2048]{0:T(1024)}, f32[2048]{0:T(1024)S(1)}, u32[]{:S(2)}) copy-start(f32[2048]{0:T(1024)S(1)} %add_rsqrt_fusion) | copy-start | bytes 24580
  23.3 20.9 %copy-start.3 = (bf16[1,2048,1024]{2,1,0:T(8,128)(2,1)S(1)}, bf16[1,2048,1024]{2,1,0:T(8,128)(2,1)}, u32[]{:S(2)}) copy-start(bf16[1,2048,1024]{2,1,0:T(8,128)(2,1)} %param.11) | copy-start | bytes 12582916
  119.4 23.3 %copy-start.4 = (f32[2048]{0:T(1024)}, f32[2048]{0:T(1024)S(1)}, u32[]{:S(2)}) copy-start(f32[2048]{0:T(1024)S(1)} %get-tuple-element.26) | copy-start | bytes 24580
  181.7 22.6 %copy-start.2 = (bf16[2048,1024]{0,1:T(8,128)(2,1)S(1)}, bf16[2048,1024]{0,1:T(8,128)(2,1)}, u32[]{:S(2)}) copy-start(bf16[2048,1024]{0,1:T(8,128)(2,1)} %get-tuple-element.27) | copy-start | bytes 12582916
  275.6 22.8 %copy-start.5 = (f32[2048]{0:T(1024)S(1)}, f32[2048]{0:T(1024)}, u32[]{:S(2)}) copy-start(f32[2048]{0:T(1024)} %copy-done.4) | copy-start | bytes 24580
  275.6 22.8 %copy-start = (bf16[1,2048,1024]{1,2,0:T(8,128)(2,1)S(1)}, bf16[1,2048,1024]{1,2,0:T(8,128)(2,1)}, u32[]{:S(2)}) copy-start(bf16[1,2048,1024]{1,2,0:T(8,128)(2,1)} %copy.21) | copy-start | bytes 12582916
  326.2 21.2 %copy-start.1 = (bf16[1,2048,1024]{1,2,0:T(8,128)(2,1)S(1)}, bf16[1,2048,1024]{1,2,0:T(8,128)(2,1)}, u32[]{:S(2)}) copy-start(bf16[1,2048,1024]{1,2,0:T(8,128)(2,1)} %copy.20) | copy-start | bytes 12582916
  326.2 21.2 %copy-start.7 = (f32[2048]{0:T(1024)S(1)}, f32[2048]{0:T(1024)}, u32[]{:S(2)}) copy-start(f32[2048]{0:T(1024)} %copy-done.6) | copy-start | bytes 24580
Sparse Core Ops, SparseCore 0:
  401.3 756.0 all-reduce.2
where the time goes:
time: 1320 us; the launch traced here: 1310 us
  waiting for transfers between devices  756 us (57%)
  matrix products  371 us (28%)
  other arithmetic  151 us (11%)
  between operations  14.3 us (1%)
    psum x1, waiting for transfers between devices, step(): summed[number] = [lax.psum(by_w[name], 'dp') for name in NAMES]  756 us
    convert_element_type x2, other arithmetic, adamw(): return ((w - 0.02 * step).astype(jnp.bfloat16), m, v)  141 us
    dot_general x5, matrix products, layer(): gate = jnp.dot(a, w['w_gate'], preferred_element_type=jnp.float32)  133 us
    dot_general x5, matrix products, layer(): up = jnp.dot(a, w['w_up'], preferred_element_type=jnp.float32)  127 us
    dot_general x5, matrix products, matmul(): jnp.dot(a, w, preferred_element_type=jnp.float32).astype(jnp.bfloat16)  111 us
  transfers between devices with their start and end apart: 1, of which 1 were waited for; matrix products, arithmetic and copies ran while one was open for 0% of the time, Pallas kernels for 0%

commit v1 on v0

v1 whole, which is shorter than its diff:
```python
import functools

import jax
import jax.numpy as jnp
from jax import lax
from jax.experimental import pallas as pl
from jax.experimental.pallas import tpu as pltpu
from jax.sharding import PartitionSpec as P

BF16, F32 = jnp.bfloat16, jnp.float32
MESH = pl.DeviceIdType.MESH
VMEM_LIMIT = 66_000_000
BLOCKS = 5
ALL = 6 * BLOCKS
SUMMED = 26
UNITS = 5
FIRST = 8
SLOTS, SEND_SLOTS, LOAD_SLOTS = 16, 8, 4
NN = (((1,), (0,)), ((), ()))
NT = (((1,), (1,)), ((), ()))


def dot(a, b, dims=NN):
    return lax.dot_general(a, b, dims, preferred_element_type=F32)


def scale_of(wide):
    return lax.rsqrt(jnp.mean(wide * wide, -1, keepdims=True) + 1e-6)


def cuts(n, width):
    starts = list(range(0, n - width + 1, width))
    return [(s, (starts[i + 1] if i + 1 < len(starts) else n) - s) for i, s in enumerate(starts)]


def forward_kernel(width, x_ref, wg_hbm, wu_hbm, wd_hbm, a0_ref, h1_ref, a1_ref, wg, wu, wd, p, sems):
    first = pl.program_id(0) == 0
    pieces = cuts(wg.shape[1], width)

    def loads(i):
        s, n = pieces[i]
        return (
            pltpu.make_async_copy(wg_hbm.at[0, :, pl.ds(s, n)], wg.at[:, pl.ds(s, n)], sems.at[0, i]),
            pltpu.make_async_copy(wu_hbm.at[0, :, pl.ds(s, n)], wu.at[:, pl.ds(s, n)], sems.at[1, i]),
            pltpu.make_async_copy(wd_hbm.at[0, pl.ds(s, n), :], wd.at[pl.ds(s, n), :], sems.at[2, i]),
        )

    @pl.when(first)
    def _():
        for i in range(len(pieces)):
            for c in loads(i)[:2]:
                c.start()
        for i in range(len(pieces)):
            loads(i)[2].start()

    wide = x_ref[...].astype(F32)
    a = (wide * scale_of(wide)).astype(BF16)
    a0_ref[...] = a
    for i, (s, n) in enumerate(pieces):

        @pl.when(first)
        def _(i=i):
            for c in loads(i)[:2]:
                c.wait()

        gate = dot(a, wg[:, s : s + n])
        up = dot(a, wu[:, s : s + n])
        p[:, s : s + n] = (gate * (0.5 * jnp.tanh(0.5 * gate) + 0.5) * up).astype(BF16)

    @pl.when(first)
    def _():
        for i in range(len(pieces)):
            loads(i)[2].wait()

    h1 = (wide + dot(p[...], wd[...]).astype(BF16).astype(F32)).astype(BF16)
    h1_ref[...] = h1
    wide1 = h1.astype(F32)
    a1_ref[...] = (wide1 * scale_of(wide1)).astype(BF16)


def forward(x, wg, wu, wd):
    t, d = x.shape
    ff = wg.shape[2]
    tile = min(t, 512)
    width = min(ff, 768)
    rows = pl.BlockSpec((tile, d), lambda i: (i, 0))
    anywhere = pl.BlockSpec(memory_space=pl.ANY)
    return pl.pallas_call(
        functools.partial(forward_kernel, width),
        grid=(t // tile,),
        out_shape=[jax.ShapeDtypeStruct((t, d), BF16)] * 3,
        in_specs=[rows, anywhere, anywhere, anywhere],
        out_specs=[rows] * 3,
        scratch_shapes=[
            pltpu.VMEM((d, ff), BF16),
            pltpu.VMEM((d, ff), BF16),
            pltpu.VMEM((ff, d), BF16),
            pltpu.VMEM((tile, ff), BF16),
            pltpu.SemaphoreType.DMA((3, len(cuts(ff, width)))),
        ],
        compiler_params=pltpu.CompilerParams(vmem_limit_bytes=VMEM_LIMIT, dimension_semantics=("arbitrary",)),
        cost_estimate=pl.CostEstimate(flops=6 * t * d * ff, bytes_accessed=6 * d * ff + 8 * t * d, transcendentals=t * ff),
        name="forward",
    )(x, wg, wu, wd)


BLOCK_STEPS, LOW_STEPS = 7, 5
TURN = BLOCKS * BLOCK_STEPS
STEPS = TURN + 1 + BLOCKS * LOW_STEPS


def step_of(s):
    low = s - (TURN + 1)
    block = jnp.where(s < TURN, s // BLOCK_STEPS, jnp.where(s == TURN, BLOCKS, BLOCKS + low // LOW_STEPS))
    kind = jnp.where(s < TURN, s % BLOCK_STEPS, jnp.where(s == TURN, 7, low % LOW_STEPS))
    return block, kind


def backward_kernel(
    a1_hbm, a0_hbm, h1_hbm, dy_hbm, wg_hbm, wu_hbm, wd_hbm,
    g_hbm, left_hbm, mine_hbm, theirs_hbm,
    ad, pgu, wgb, wub, wdb, wgt, wut, dat, stage, mb, xb, sb, ra, rb, tot,
    in_sem, w_sem, own_sem, give_sem, get_sem, left_sem, load_sem, s_sem, ra_sem, rb_sem, tot_sem, down_sem, up_sem, keep_sem, pass_sem, partner_sem,
):
    me = lax.axis_index("dp")
    z, core = me // 2, me % 2
    partner = me + 1 - 2 * core
    t, d = ad.shape[1:]
    f = stage.shape[1]
    half, r = f // 2, f // 2 // UNITS
    units = SUMMED * UNITS
    sub = dat.shape[2]

    def remote(src, dst, send, recv, device):
        return pltpu.make_async_remote_copy(src_ref=src, dst_ref=dst, send_sem=send, recv_sem=recv, device_id={"dp": device}, device_id_type=MESH)

    barrier = pltpu.get_barrier_semaphore()
    pl.semaphore_signal(barrier, inc=1, device_id={"dp": partner}, device_id_type=MESH)

    @pl.when(z > 0)
    def _():
        pl.semaphore_signal(barrier, inc=1, device_id={"dp": me - 2}, device_id_type=MESH)

    @pl.when(z < 3)
    def _():
        pl.semaphore_signal(barrier, inc=1, device_id={"dp": me + 2}, device_id_type=MESH)

    pl.semaphore_wait(barrier, 3 - z // 3 - (3 - z) // 3)

    def weights(block):
        layer, j, slot = 1 - block // BLOCKS, block % BLOCKS, block % 2
        at = pl.ds(pl.multiple_of(j * f, f), f)
        return (
            pltpu.make_async_copy(wg_hbm.at[layer, :, at], wgb.at[slot], w_sem.at[slot, 0]),
            pltpu.make_async_copy(wu_hbm.at[layer, :, at], wub.at[slot], w_sem.at[slot, 1]),
            pltpu.make_async_copy(wd_hbm.at[layer, at, :], wdb.at[slot], w_sem.at[slot, 2]),
        )

    load_dy = pltpu.make_async_copy(dy_hbm, ad.at[0], in_sem.at[0])
    load_a1 = pltpu.make_async_copy(a1_hbm, ad.at[1], in_sem.at[1])
    load_h1 = pltpu.make_async_copy(h1_hbm, ad.at[1], in_sem.at[2])
    load_a0 = pltpu.make_async_copy(a0_hbm, ad.at[1], in_sem.at[3])

    def hidden(block, kind):
        slot = block % 2

        @pl.when(kind == 0)
        def _():
            @pl.when(block == 0)
            def _():
                load_dy.wait()
                load_a1.wait()

            @pl.when(block == BLOCKS)
            def _():
                load_a0.wait()

            for c in weights(block):
                c.wait()

            @pl.when(block + 1 < 2 * BLOCKS)
            def _():
                for c in weights(block + 1):
                    c.start()

            wgt[...] = wgb[slot].T
            wut[...] = wub[slot].T

        for i in range(t // 2 // sub):
            at = pl.ds(pl.multiple_of(kind * (t // 2) + i * sub, sub), sub)
            gate = dot(wgt[...], ad[1, at, :], NT)
            up = dot(wut[...], ad[1, at, :], NT)
            dp = dot(wdb[slot], ad[0, at, :], NT).astype(BF16).astype(F32)
            sig = 0.5 * jnp.tanh(0.5 * gate) + 0.5
            silu = gate * sig
            pgu[0, :, at] = (silu * up).astype(BF16)
            pgu[1, :, at] = (dp * up * (sig + silu * (1.0 - sig))).astype(BF16)
            pgu[2, :, at] = (dp * silu).astype(BF16)

    def gradient(block, kind):
        which = kind - 2
        slot = (3 * block + which) % 2
        rhs = jnp.minimum(which, 1)
        lhs = pgu[which]
        for i in range(2):
            cols = slice(i * (d // 2), (i + 1) * (d // 2))
            stage[slot, :, cols] = dot(lhs, ad[rhs, :, cols]).astype(BF16)

    def to_input(block, kind):
        slot = block % 2

        @pl.when((block == BLOCKS - 1) & (kind == 5))
        def _():
            load_h1.start()

        for i in range(t // 2 // sub):
            tile = (kind - 5) * (t // 2 // sub) + i
            at = pl.ds(pl.multiple_of(tile * sub, sub), sub)
            dat[tile] += dot(wgb[slot], pgu[1, :, at]) + dot(wub[slot], pgu[2, :, at])

    def turn():
        load_h1.wait()

        def body(i, _):
            at = pl.ds(pl.multiple_of(i * sub, sub), sub)
            da = dat[i].T.astype(BF16).astype(F32)
            wide = ad[1, at, :].astype(F32)
            scale = scale_of(wide)
            inner = jnp.sum(da * wide, -1, keepdims=True) * (scale * scale * scale) * (1.0 / d)
            through = (da * scale - wide * inner).astype(BF16).astype(F32)
            ad[0, at, :] = (ad[0, at, :].astype(F32) + through).astype(BF16)
            return 0

        lax.fori_loop(0, t // sub, body, 0)
        load_a0.start()

    def rows(slot, c):
        return stage.at[slot, pl.ds(pl.multiple_of(c * half, half), half), :]

    def piece_copies(q):
        slot = q % 2
        own = pltpu.make_async_copy(rows(slot, core), mine_hbm.at[q], own_sem.at[q])
        give = remote(rows(slot, 1 - core), theirs_hbm.at[q], give_sem.at[slot], get_sem.at[q], partner)
        return own, give

    def left_copy(q):
        return pltpu.make_async_copy(stage.at[q % 2], left_hbm.at[q - SUMMED], left_sem.at[q % 2])

    def send_stage(q):
        @pl.when(q < SUMMED)
        def _():
            own, give = piece_copies(q)
            own.start()
            give.start()

        @pl.when(q >= SUMMED)
        def _():
            left_copy(q).start()

    def wait_stage(q):
        @pl.when(q < SUMMED)
        def _():
            own, give = piece_copies(q)
            own.wait()
            give.wait_send()

        @pl.when(q >= SUMMED)
        def _():
            left_copy(q).wait()

    is0, is1, is2, is3 = z == 0, z == 1, z == 2, z == 3
    sum_lag = jnp.where(is1, 4, jnp.where(is2, 2, 0))
    tot_lag = jnp.where(is1, 4, jnp.where(is3, 10, 7))
    free_lag = tot_lag + jnp.where(is3, 3, 4)

    def load_copies(k):
        q, at, slot = k // UNITS, pl.ds(pl.multiple_of((k % UNITS) * r, r), r), k % LOAD_SLOTS
        return (
            pltpu.make_async_copy(mine_hbm.at[q, at, :], mb.at[slot], load_sem.at[slot, 0]),
            pltpu.make_async_copy(theirs_hbm.at[q, at, :], xb.at[slot], load_sem.at[slot, 1]),
        )

    def s_copy_edge(k):
        return remote(sb.at[k % SEND_SLOTS], ra.at[k % SLOTS], s_sem.at[k % SEND_SLOTS], ra_sem.at[k % SLOTS], me + 2 - 4 * (z // 3))

    def s_copy_inner(k):
        return remote(sb.at[k % SEND_SLOTS], rb.at[k % SLOTS], s_sem.at[k % SEND_SLOTS], rb_sem.at[k % SLOTS], me - 2)

    def tot_down(k):
        return remote(tot.at[k % SLOTS], tot.at[k % SLOTS], down_sem.at[k % SLOTS], tot_sem.at[k % SLOTS], me - 2)

    def tot_up(k):
        return remote(tot.at[k % SLOTS], tot.at[k % SLOTS], up_sem.at[k % SLOTS], tot_sem.at[k % SLOTS], me + 2)

    def out_copies(k):
        q, at, slot = k // UNITS, pl.ds(pl.multiple_of(core * half + (k % UNITS) * r, r), r), k % SLOTS
        return (
            pltpu.make_async_copy(tot.at[slot], g_hbm.at[q, at, :], keep_sem.at[slot]),
            remote(tot.at[slot], g_hbm.at[q, at, :], pass_sem.at[slot], partner_sem, partner),
        )

    def inside(k):
        return (k >= 0) & (k < units)

    def free(k):
        @pl.when(inside(k))
        def _():
            keep, give = out_copies(k)
            keep.wait()
            give.wait_send()

            @pl.when(is1)
            def _():
                tot_down(k).wait_send()

            @pl.when(is1 | is2)
            def _():
                tot_up(k).wait_send()

    def add(k):
        @pl.when(inside(k))
        def _():
            for c in load_copies(k):
                c.wait()
            slot = k % LOAD_SLOTS
            both = mb[slot].astype(F32) + xb[slot].astype(F32)

            @pl.when((is0 | is3) & (k >= SEND_SLOTS))
            def _():
                s_copy_edge(k - SEND_SLOTS).wait_send()

            @pl.when(is2 & (k >= SEND_SLOTS))
            def _():
                s_copy_inner(k - SEND_SLOTS).wait_send()

            @pl.when(is0 | is3)
            def _():
                sb[k % SEND_SLOTS] = both.astype(BF16)

            @pl.when(is2)
            def _():
                s_copy_edge(k).wait_recv()
                sb[k % SEND_SLOTS] = (both + ra[k % SLOTS].astype(F32)).astype(BF16)

            @pl.when(is1)
            def _():
                s_copy_edge(k).wait_recv()
                s_copy_inner(k).wait_recv()
                tot[k % SLOTS] = (both + ra[k % SLOTS].astype(F32) + rb[k % SLOTS].astype(F32)).astype(BF16)

    def arrive(k):
        @pl.when(inside(k) & (z != 1))
        def _():
            tot_down(k).wait_recv()

    def send(k_sum, k_tot):
        @pl.when(inside(k_sum) & (is0 | is3))
        def _():
            s_copy_edge(k_sum).start()

        @pl.when(inside(k_sum) & is2)
        def _():
            s_copy_inner(k_sum).start()

        @pl.when(inside(k_tot))
        def _():
            @pl.when(is1)
            def _():
                tot_down(k_tot).start()

            @pl.when(is1 | is2)
            def _():
                tot_up(k_tot).start()

            for c in out_copies(k_tot):
                c.start()

    def load(k):
        @pl.when(inside(k))
        def _():
            @pl.when(k % UNITS == 0)
            def _():
                piece_copies(k // UNITS)[1].wait_recv()

            for c in load_copies(k):
                c.start()

    load_dy.start()
    load_a1.start()
    for c in weights(0):
        c.start()
    dat[...] = jnp.zeros_like(dat)

    def tick(i, _):
        step = i // 2
        works = i % 2 == 0

        @pl.when((step >= 1) & (step <= STEPS))
        def _():
            block, kind = step_of(step - 1)
            q = 3 * block + kind - 2

            @pl.when((kind >= 2) & (kind <= 4) & works)
            def _():
                send_stage(q)

            @pl.when((kind >= 2) & (kind <= 4) & (i % 2 == 1))
            def _():
                wait_stage(q)

        now = i - FIRST
        free(now - free_lag)
        add(now - sum_lag)
        arrive(now - tot_lag)
        send(now - sum_lag, now - tot_lag)
        load(now - sum_lag + 1)

        @pl.when(works & (step < STEPS))
        def _():
            block, kind = step_of(step)

            @pl.when(kind <= 1)
            def _():
                hidden(block, kind)

            @pl.when((kind >= 2) & (kind <= 4))
            def _():
                gradient(block, kind)

            @pl.when((kind == 5) | (kind == 6))
            def _():
                to_input(block, kind)

            @pl.when(kind == 7)
            def _():
                turn()

        return 0

    lax.fori_loop(0, max(FIRST + units + 14, 2 * STEPS + 2), tick, 0)

    for k in range(units - SEND_SLOTS, units):

        @pl.when(is0 | is3)
        def _(k=k):
            s_copy_edge(k).wait_send()

        @pl.when(is2)
        def _(k=k):
            s_copy_inner(k).wait_send()

    pltpu.make_async_copy(theirs_hbm, theirs_hbm, partner_sem).wait()


def backward(a1, a0, h1, dy, wg, wu, wd):
    t, d = a1.shape
    ff = wg.shape[2]
    f = ff // BLOCKS
    r = f // 2 // UNITS
    sub = t // 4
    anywhere = pl.BlockSpec(memory_space=pl.ANY)
    dma = pltpu.SemaphoreType.DMA
    return pl.pallas_call(
        backward_kernel,
        out_shape=[
            jax.ShapeDtypeStruct((SUMMED, f, d), BF16),
            jax.ShapeDtypeStruct((ALL - SUMMED, f, d), BF16),
            jax.ShapeDtypeStruct((SUMMED, f // 2, d), BF16),
            jax.ShapeDtypeStruct((SUMMED, f // 2, d), BF16),
        ],
        in_specs=[anywhere] * 7,
        out_specs=[anywhere] * 4,
        scratch_shapes=[
            pltpu.VMEM((2, t, d), BF16),
            pltpu.VMEM((3, f, t), BF16),
            pltpu.VMEM((2, d, f), BF16),
            pltpu.VMEM((2, d, f), BF16),
            pltpu.VMEM((2, f, d), BF16),
            pltpu.VMEM((f, d), BF16),
            pltpu.VMEM((f, d), BF16),
            pltpu.VMEM((4, d, sub), F32),
            pltpu.VMEM((2, f, d), BF16),
            pltpu.VMEM((LOAD_SLOTS, r, d), BF16),
            pltpu.VMEM((LOAD_SLOTS, r, d), BF16),
            pltpu.VMEM((SEND_SLOTS, r, d), BF16),
            pltpu.VMEM((SLOTS, r, d), BF16),
            pltpu.VMEM((SLOTS, r, d), BF16),
            pltpu.VMEM((SLOTS, r, d), BF16),
            dma((4,)),
            dma((2, 3)),
            dma((SUMMED,)),
            dma((2,)),
            dma((SUMMED,)),
            dma((2,)),
            dma((LOAD_SLOTS, 2)),
            dma((SEND_SLOTS,)),
            dma((SLOTS,)),
            dma((SLOTS,)),
            dma((SLOTS,)),
            dma((SLOTS,)),
            dma((SLOTS,)),
            dma((SLOTS,)),
            dma((SLOTS,)),
            dma,
        ],
        compiler_params=pltpu.CompilerParams(collective_id=0, has_side_effects=True, vmem_limit_bytes=VMEM_LIMIT),
        cost_estimate=pl.CostEstimate(flops=2 * 15 * t * d * ff, bytes_accessed=100 * d * ff, transcendentals=2 * t * ff),
        name="backward",
    )(a1, a0, h1, dy, wg, wu, wd)


def adamw_kernel(turned, n_old, w_ref, m_ref, v_ref, g_ref, *rest):
    w_out, m_out, v_out = rest[n_old:]
    g = g_ref[0].astype(F32)
    if turned:
        g = g.T
    m = 0.9 * m_ref[0] + 0.1 * g
    v = 0.95 * v_ref[0] + 0.05 * g * g
    w = w_ref[0].astype(F32)
    w_out[0] = (w - 0.02 * (m * lax.rsqrt(v + 1e-8) + 0.1 * w)).astype(BF16)
    m_out[0] = m
    v_out[0] = v


def adamw(which, blocks, first, g, w, m, v, old=()):
    low, high = blocks
    turned = which > 0
    d = min(w.shape[1], w.shape[2])
    f = max(w.shape[1], w.shape[2]) // BLOCKS

    def place(i, s):
        b = low + i
        layer, j = 1 - b // BLOCKS, b % BLOCKS
        return (layer, s, j) if turned else (layer, 2 * j + s, 0)

    if turned:
        spec = pl.BlockSpec((1, d // 2, f), place)
        g_spec = pl.BlockSpec((1, f, d // 2), lambda i, s: (3 * (low + i) + which - first, 0, s))
    else:
        spec = pl.BlockSpec((1, f // 2, d), place)
        g_spec = pl.BlockSpec((1, f // 2, d), lambda i, s: (3 * (low + i) + which - first, s, 0))
    n = (high - low) * d * f
    return pl.pallas_call(
        functools.partial(adamw_kernel, turned, len(old)),
        grid=(high - low, 2),
        out_shape=[jax.ShapeDtypeStruct(w.shape, BF16), jax.ShapeDtypeStruct(w.shape, F32), jax.ShapeDtypeStruct(w.shape, F32)],
        in_specs=[spec, spec, spec, g_spec] + [pl.BlockSpec(memory_space=pl.ANY)] * len(old),
        out_specs=[spec] * 3,
        input_output_aliases={4 + i: i for i in range(len(old))},
        compiler_params=pltpu.CompilerParams(vmem_limit_bytes=VMEM_LIMIT, dimension_semantics=("arbitrary", "arbitrary")),
        cost_estimate=pl.CostEstimate(flops=2000 * n, bytes_accessed=22 * n, transcendentals=n),
        name=f"adamw_{which}",
    )(w, m, v, g, *old)


def solution(mesh):
    def step(x, dy, *arrays):
        w, m, v = (arrays[i : i + 3] for i in (0, 3, 6))
        wg, wu, wd = w
        a0, h1, a1 = forward(x[0], wg, wu, wd)
        g, left, _, _ = backward(a1, a0, h1, dy[0], wg, wu, wd)
        left = lax.psum(left, "dp")
        new = []
        for name, which in ((0, 1), (1, 2), (2, 0)):
            done = (SUMMED - which + 2) // 3
            first = adamw(which, (0, done), 0, g, w[name], m[name], v[name])
            new.append((done, which, name, first))
        out = [adamw(which, (done, 2 * BLOCKS), SUMMED, left, w[name], m[name], v[name], first) for done, which, name, first in new]
        return tuple(one[kind] for kind in range(3) for one in out)

    return jax.shard_map(
        step,
        mesh=mesh,
        in_specs=(P(("rep", "dp"), None, None),) * 2 + (P(None, None, None),) * 9,
        out_specs=(P("rep", None, None),) * 9,
        check_vma=False,
    )
```

time: 1320 us -> 650 us (0.49)
  waiting for transfers between devices: 756 us -> 0.03 us
  Pallas kernels: 0 us -> 634 us
  matrix products: 371 us -> 0 us
  other arithmetic: 151 us -> 0 us
    psum x1, waiting for transfers between devices: 756 us -> 0.01 us  [step(): left = lax.psum(left, 'dp')]
    pallas_call x0 -> x8, Pallas kernels: none -> 634 us  [the longest x1 422 us: backward(): pl.pallas_call(backward_kernel, out_shape=[jax.ShapeDtypeStruct((SUMMED,...]
    dot_general x15 -> x0, matrix products: 371 us -> none  [the longest x5 133 us: layer(): gate = jnp.dot(a, w['w_gate'], preferred_element_type=jnp.float32)]
    convert_element_type x2 -> x0, other arithmetic: 141 us -> none  [adamw(): return ((w - 0.02 * step).astype(jnp.bfloat16), m, v)]
  transfers between devices with their start and end apart: 1 -> 1, of which waited for: 1 -> 0; matrix products, arithmetic and copies ran while one was open for 0% -> 0% of each run, Pallas kernels for 0% -> 21%
where the time goes in v1:
time: 650 us; the launch traced here: 648 us
  Pallas kernels  634 us (98%)
  between operations  14.1 us (2%)
    pallas_call x1, Pallas kernels, backward(): pl.pallas_call(backward_kernel, out_shape=[jax.ShapeDtypeStruct((SUMMED,...  422 us
    pallas_call x6, Pallas kernels, adamw(): pl.pallas_call(functools.partial(adamw_kernel, turned, len(old)), grid=(h...  159 us
    pallas_call x1, Pallas kernels, forward(): pl.pallas_call(functools.partial(forward_kernel, width), grid=(t // tile,...  52.3 us
  transfers between devices with their start and end apart: 1, of which 0 were waited for; matrix products, arithmetic and copies ran while one was open for 0% of the time, Pallas kernels for 21%

profile of v1, /device:TPU:27, one launch (start us, length us, event | category | flops | bytes accessed | tf_op | source)
XLA Modules:
  0.0 647.7 jit_solution(16619454372411992085)
XLA Ops:
  7.2 0.0 all-reduce.2.cloned.1.call-start
  7.2 52.3 %forward.1 = (bf16[2048,1024]{1,0:T(8,128)(2,1)}, bf16[2048,1024]{1,0:T(8,128)(2,1)}, bf16[2048,1024]{1,0:T(8,128)(2,1)}) custom-call(bf16[2048,1024]{1,0:T(8,128)(2,1)} %bitcast.2, bf16[2,1024,3200]{2,1,0:T(8,128)(2,1)} %w_ref.7, bf16[2,1024,3200]{2,1,0:T(8,128)(2,1)} %w_ref.9, bf16[2,3200,1024]{2,1,0:T(8,128)(2,1)} %w_ref.11), custom_call_target="tpu_custom_call" | custom-call | flops 40265318400 | bytes 36438016 | tf_op jit(solution)/shard_map/forward/pallas_call | solution.py:88
  59.6 421.8 %backward.1 = (bf16[26,640,1024]{2,1,0:T(8,128)(2,1)}, bf16[4,640,1024]{2,1,0:T(8,128)(2,1)}, bf16[26,320,1024]{2,1,0:T(8,128)(2,1)}, bf16[26,320,1024]{2,1,0:T(8,128)(2,1)}) custom-call(bf16[2048,1024]{1,0:T(8,128)(2,1)} %get-tuple-element.32.a1_hbm, bf16[2048,1024]{1,0:T(8,128)(2,1)} %get-tuple-element.33.a0_hbm, ...), custom_call_target="tpu_custom_call" | custom-call | flops 201326592000 | bytes 327680000 | tf_op jit(solution)/shard_map/backward/pallas_call | solution.py:463
  481.3 0.0 all-reduce.2.cloned.1.call-update
  481.4 42.9 %adamw_2.2 = (bf16[2,1024,3200]{2,1,0:T(8,128)(2,1)}, f32[2,1024,3200]{2,1,0:T(8,128)}, f32[2,1024,3200]{2,1,0:T(8,128)}) custom-call(bf16[2,1024,3200]{2,1,0:T(8,128)(2,1)} %w_ref.9, f32[2,1024,3200]{2,1,0:T(8,128)} %m_ref.9, f32[2,1024,3200]{2,1,0:T(8,128)} %v_ref.9, bf16[26,640,1024]{2,1,0:T(8,128)(2,1)} %get-tuple-element.36.g_ref), custom_call_target="tpu_custom_call" | custom-call | flops 10485760000 | bytes 115343360 | tf_op jit(solution)/shard_map/adamw_2/pallas_call | solution.py:543
  524.2 45.9 %adamw_0.2 = (bf16[2,3200,1024]{2,1,0:T(8,128)(2,1)}, f32[2,3200,1024]{2,1,0:T(8,128)}, f32[2,3200,1024]{2,1,0:T(8,128)}) custom-call(bf16[2,3200,1024]{2,1,0:T(8,128)(2,1)} %w_ref.11, f32[2,3200,1024]{2,1,0:T(8,128)} %m_ref.11, f32[2,3200,1024]{2,1,0:T(8,128)} %v_ref.11, bf16[26,640,1024]{2,1,0:T(8,128)(2,1)} %get-tuple-element.36.g_ref), custom_call_target="tpu_custom_call" | custom-call | flops 11796480000 | bytes 129761280 | tf_op jit(solution)/shard_map/adamw_0/pallas_call | solution.py:543
  570.2 48.4 %adamw_1.2 = (bf16[2,1024,3200]{2,1,0:T(8,128)(2,1)}, f32[2,1024,3200]{2,1,0:T(8,128)}, f32[2,1024,3200]{2,1,0:T(8,128)}) custom-call(bf16[2,1024,3200]{2,1,0:T(8,128)(2,1)} %w_ref.7, f32[2,1024,3200]{2,1,0:T(8,128)} %m_ref.7, f32[2,1024,3200]{2,1,0:T(8,128)} %v_ref.7, bf16[26,640,1024]{2,1,0:T(8,128)(2,1)} %get-tuple-element.36.g_ref), custom_call_target="tpu_custom_call" | custom-call | flops 11796480000 | bytes 129761280 | tf_op jit(solution)/shard_map/adamw_1/pallas_call | solution.py:543
  618.5 0.0 all-reduce.2.cloned.1.call-done.g_ref
  618.6 5.5 adamw_0.3
  624.1 11.1 %adamw_2.3 = (bf16[2,1024,3200]{2,1,0:T(8,128)(2,1)}, f32[2,1024,3200]{2,1,0:T(8,128)}, f32[2,1024,3200]{2,1,0:T(8,128)}) custom-call(bf16[2,1024,3200]{2,1,0:T(8,128)(2,1)} %w_ref.9, f32[2,1024,3200]{2,1,0:T(8,128)} %m_ref.9, f32[2,1024,3200]{2,1,0:T(8,128)} %v_ref.9, ...), custom_call_target="tpu_custom_call", output_to_operand_aliasing={{0}: (4, {}), {1}: (5, {}), {2}: (6, {})} | custom-call | flops 2621440000 | bytes 28835840 | tf_op jit(solution)/shard_map/adamw_2/pallas_call | solution.py:543
  635.1 5.7 adamw_1.3
Async XLA Ops:
  7.2 611.4 %all-reduce.2.cloned.1.call-start = ((), (), s32[]{:S(2)}) async-start(), calls=%async_computation | async-start | bytes 10485760 | tf_op jit(solution)/shard_map/psum | solution.py:562
Sparse Core Ops, SparseCore 0:
  481.5 115.5 all-reduce.1

commit v2 on v1

--- a/solution.py
+++ b/solution.py
@@ -53,9 +53,13 @@
         for i in range(len(pieces)):
             loads(i)[2].start()
 
+    def product(s, n, gate, up):
+        p[:, s : s + n] = (gate * (0.5 * jnp.tanh(0.5 * gate) + 0.5) * up).astype(BF16)
+
     wide = x_ref[...].astype(F32)
     a = (wide * scale_of(wide)).astype(BF16)
     a0_ref[...] = a
+    ready = None
     for i, (s, n) in enumerate(pieces):
 
         @pl.when(first)
@@ -65,14 +69,20 @@
 
         gate = dot(a, wg[:, s : s + n])
         up = dot(a, wu[:, s : s + n])
-        p[:, s : s + n] = (gate * (0.5 * jnp.tanh(0.5 * gate) + 0.5) * up).astype(BF16)
+        if ready is not None:
+            product(*ready)
+        ready = (s, n, gate, up)
 
     @pl.when(first)
     def _():
         for i in range(len(pieces)):
             loads(i)[2].wait()
 
-    h1 = (wide + dot(p[...], wd[...]).astype(BF16).astype(F32)).astype(BF16)
+    last = pieces[-1][0]
+    down = dot(p[:, :last], wd[:last, :])
+    product(*ready)
+    down += dot(p[:, last:], wd[last:, :])
+    h1 = (wide + down.astype(BF16).astype(F32)).astype(BF16)
     h1_ref[...] = h1
     wide1 = h1.astype(F32)
     a1_ref[...] = (wide1 * scale_of(wide1)).astype(BF16)
@@ -134,19 +144,6 @@
     def remote(src, dst, send, recv, device):
         return pltpu.make_async_remote_copy(src_ref=src, dst_ref=dst, send_sem=send, recv_sem=recv, device_id={"dp": device}, device_id_type=MESH)
 
-    barrier = pltpu.get_barrier_semaphore()
-    pl.semaphore_signal(barrier, inc=1, device_id={"dp": partner}, device_id_type=MESH)
-
-    @pl.when(z > 0)
-    def _():
-        pl.semaphore_signal(barrier, inc=1, device_id={"dp": me - 2}, device_id_type=MESH)
-
-    @pl.when(z < 3)
-    def _():
-        pl.semaphore_signal(barrier, inc=1, device_id={"dp": me + 2}, device_id_type=MESH)
-
-    pl.semaphore_wait(barrier, 3 - z // 3 - (3 - z) // 3)
-
     def weights(block):
         layer, j, slot = 1 - block // BLOCKS, block % BLOCKS, block % 2
         at = pl.ds(pl.multiple_of(j * f, f), f)
@@ -160,6 +157,25 @@
     load_a1 = pltpu.make_async_copy(a1_hbm, ad.at[1], in_sem.at[1])
     load_h1 = pltpu.make_async_copy(h1_hbm, ad.at[1], in_sem.at[2])
     load_a0 = pltpu.make_async_copy(a0_hbm, ad.at[1], in_sem.at[3])
+
+    load_a1.start()
+    for c in weights(0):
+        c.start()
+    load_dy.start()
+    dat[...] = jnp.zeros_like(dat)
+
+    barrier = pltpu.get_barrier_semaphore()
+    pl.semaphore_signal(barrier, inc=1, device_id={"dp": partner}, device_id_type=MESH)
+
+    @pl.when(z > 0)
+    def _():
+        pl.semaphore_signal(barrier, inc=1, device_id={"dp": me - 2}, device_id_type=MESH)
+
+    @pl.when(z < 3)
+    def _():
+        pl.semaphore_signal(barrier, inc=1, device_id={"dp": me + 2}, device_id_type=MESH)
+
+    pl.semaphore_wait(barrier, 3 - z // 3 - (3 - z) // 3)
 
     def hidden(block, kind):
         slot = block % 2
@@ -385,11 +401,6 @@
             for c in load_copies(k):
                 c.start()
 
-    load_dy.start()
-    load_a1.start()
-    for c in weights(0):
-        c.start()
-    dat[...] = jnp.zeros_like(dat)
 
     def tick(i, _):
         step = i // 2
@@ -509,48 +520,169 @@
     )(a1, a0, h1, dy, wg, wu, wd)
 
 
-def adamw_kernel(turned, n_old, w_ref, m_ref, v_ref, g_ref, *rest):
-    w_out, m_out, v_out = rest[n_old:]
-    g = g_ref[0].astype(F32)
-    if turned:
-        g = g.T
-    m = 0.9 * m_ref[0] + 0.1 * g
-    v = 0.95 * v_ref[0] + 0.05 * g * g
-    w = w_ref[0].astype(F32)
-    w_out[0] = (w - 0.02 * (m * lax.rsqrt(v + 1e-8) + 0.1 * w)).astype(BF16)
-    m_out[0] = m
-    v_out[0] = v
-
-
-def adamw(which, blocks, first, g, w, m, v, old=()):
-    low, high = blocks
-    turned = which > 0
-    d = min(w.shape[1], w.shape[2])
-    f = max(w.shape[1], w.shape[2]) // BLOCKS
-
-    def place(i, s):
-        b = low + i
-        layer, j = 1 - b // BLOCKS, b % BLOCKS
-        return (layer, s, j) if turned else (layer, 2 * j + s, 0)
-
-    if turned:
-        spec = pl.BlockSpec((1, d // 2, f), place)
-        g_spec = pl.BlockSpec((1, f, d // 2), lambda i, s: (3 * (low + i) + which - first, 0, s))
-    else:
-        spec = pl.BlockSpec((1, f // 2, d), place)
-        g_spec = pl.BlockSpec((1, f // 2, d), lambda i, s: (3 * (low + i) + which - first, s, 0))
+HALVES = ((1, 0), (1, 1), (2, 0), (2, 1), (0, 0), (0, 1))
+
+
+def adamw_kernel(rounds, first, n_old, *refs):
+    arrays = {1: refs[0:3], 2: refs[3:6], 0: refs[6:9]}
+    g_hbm = refs[9]
+    outs = refs[10 + n_old :][:9]
+    outs = {1: outs[0:3], 2: outs[3:6], 0: outs[6:9]}
+    wt, mt, vt, gt, wd, md, vd, gd, wt_out, mt_out, vt_out, wd_out, md_out, vd_out, turned, in_sem, out_sem = refs[10 + n_old + 9 :]
+    d, f = wt.shape[1] * 2, wt.shape[2]
+
+    def place(b, half):
+        which, s = HALVES[half]
+        layer, j, q = 1 - b // BLOCKS, b % BLOCKS, 3 * b + which - first
+        if which:
+            cols = pl.ds(pl.multiple_of(j * f, f), f)
+            return which, lambda ref: ref.at[layer, pl.ds(s * (d // 2), d // 2), cols], g_hbm.at[q, :, pl.ds(s * (d // 2), d // 2)]
+        rows = pl.ds(pl.multiple_of(j * f + s * (f // 2), f // 2), f // 2)
+        return which, lambda ref: ref.at[layer, rows, :], g_hbm.at[q, pl.ds(s * (f // 2), f // 2), :]
+
+    def buffers(half):
+        if HALVES[half][0]:
+            return [x.at[half] for x in (wt, mt, vt, gt)], [x.at[half] for x in (wt_out, mt_out, vt_out)]
+        return [x.at[half - 4] for x in (wd, md, vd, gd)], [x.at[half - 4] for x in (wd_out, md_out, vd_out)]
+
+    def loads(b, half):
+        which, at, g = place(b, half)
+        sources = [at(x) for x in arrays[which]] + [g]
+        return [pltpu.make_async_copy(x, y, in_sem.at[half, i]) for i, (x, y) in enumerate(zip(sources, buffers(half)[0], strict=True))]
+
+    def stores(b, half):
+        which, at, _ = place(b, half)
+        return [pltpu.make_async_copy(x, at(y), out_sem.at[half, i]) for i, (x, y) in enumerate(zip(buffers(half)[1], outs[which], strict=True))]
+
+    def take(half):
+        (w_in, m_in, v_in, g_in), (w_out, m_out, v_out) = buffers(half)
+        if HALVES[half][0]:
+            turned[...] = g_in[...].T
+            g_in = turned
+
+        def body(i, _):
+            at = pl.ds(pl.multiple_of(i * 16, 16), 16)
+            g = g_in[at, :].astype(F32)
+            m = 0.9 * m_in[at, :] + 0.1 * g
+            v = 0.95 * v_in[at, :] + 0.05 * g * g
+            w = w_in[at, :].astype(F32)
+            w_out[at, :] = (w - 0.02 * (m * lax.rsqrt(v + 1e-8) + 0.1 * w)).astype(BF16)
+            m_out[at, :] = m
+            v_out[at, :] = v
+            return 0
+
+        lax.fori_loop(0, w_in.shape[0] // 16, body, 0, unroll=2)
+
+    def start(copies):
+        for c in copies:
+            c.start()
+
+    def wait(copies):
+        for c in copies:
+            c.wait()
+
+    starts = {}
+    for blocks, halves in rounds:
+        for half in halves:
+            if half not in starts:
+                starts[half] = True
+                start(loads(blocks[0], half))
+    before = {}
+    for n, (blocks, halves) in enumerate(rounds):
+        low, high = blocks
+
+        def next_of(half, n=n):
+            return next((bs[0] for bs, hs in rounds[n + 1 :] if half in hs), None)
+
+        def one(b, half, low=low, high=high, next_of=next_of):
+            wait(loads(b, half))
+            if half in before:
+                wait(stores(before[half], half))
+            elif high - low > 1:
+
+                @pl.when(b > low)
+                def _():
+                    wait(stores(b - 1, half))
+
+            take(half)
+            start(stores(b, half))
+            if high - low > 1:
+
+                @pl.when(b + 1 < high)
+                def _():
+                    start(loads(b + 1, half))
+
+            after = next_of(half)
+            if after is not None:
+                if high - low > 1:
+
+                    @pl.when(b + 1 == high)
+                    def _():
+                        start(loads(after, half))
+
+                else:
+                    start(loads(after, half))
+
+        def turn(b, _, halves=halves):
+            for half in halves:
+                one(b, half)
+            return 0
+
+        if high - low > 1:
+            lax.fori_loop(low, high, turn, 0)
+        else:
+            turn(low, 0)
+        for half in halves:
+            before[half] = high - 1
+    for half, b in before.items():
+        wait(stores(b, half))
+
+
+def adamw(pieces, first, g, w, m, v, old=()):
+    low, high = pieces
+    d, ff = w[0].shape[1:]
+    f = ff // BLOCKS
+    rounds = []
+    for b in range(2 * BLOCKS):
+        halves = tuple(h for h, (which, _) in enumerate(HALVES) if low <= 3 * b + which < high)
+        if not halves:
+            continue
+        if len(rounds) == 1 and rounds[0][1] == halves:
+            rounds[-1] = ((rounds[-1][0][0], b + 1), halves)
+        else:
+            rounds.append(((b, b + 1), halves))
+    anywhere = pl.BlockSpec(memory_space=pl.ANY)
+    operands = [x for i in range(3) for x in (w[i], m[i], v[i])]
     n = (high - low) * d * f
     return pl.pallas_call(
-        functools.partial(adamw_kernel, turned, len(old)),
-        grid=(high - low, 2),
-        out_shape=[jax.ShapeDtypeStruct(w.shape, BF16), jax.ShapeDtypeStruct(w.shape, F32), jax.ShapeDtypeStruct(w.shape, F32)],
-        in_specs=[spec, spec, spec, g_spec] + [pl.BlockSpec(memory_space=pl.ANY)] * len(old),
-        out_specs=[spec] * 3,
-        input_output_aliases={4 + i: i for i in range(len(old))},
-        compiler_params=pltpu.CompilerParams(vmem_limit_bytes=VMEM_LIMIT, dimension_semantics=("arbitrary", "arbitrary")),
+        functools.partial(adamw_kernel, tuple(rounds), first, len(old)),
+        out_shape=[jax.ShapeDtypeStruct(x.shape, x.dtype) for x in operands],
+        in_specs=[anywhere] * (10 + len(old)),
+        out_specs=[anywhere] * 9,
+        scratch_shapes=[
+            pltpu.VMEM((4, d // 2, f), BF16),
+            pltpu.VMEM((4, d // 2, f), F32),
+            pltpu.VMEM((4, d // 2, f), F32),
+            pltpu.VMEM((4, f, d // 2), BF16),
+            pltpu.VMEM((2, f // 2, d), BF16),
+            pltpu.VMEM((2, f // 2, d), F32),
+            pltpu.VMEM((2, f // 2, d), F32),
+            pltpu.VMEM((2, f // 2, d), BF16),
+            pltpu.VMEM((4, d // 2, f), BF16),
+            pltpu.VMEM((4, d // 2, f), F32),
+            pltpu.VMEM((4, d // 2, f), F32),
+            pltpu.VMEM((2, f // 2, d), BF16),
+            pltpu.VMEM((2, f // 2, d), F32),
+            pltpu.VMEM((2, f // 2, d), F32),
+            pltpu.VMEM((d // 2, f), BF16),
+            pltpu.SemaphoreType.DMA((6, 4)),
+            pltpu.SemaphoreType.DMA((6, 3)),
+        ],
+        input_output_aliases={10 + i: i for i in range(len(old))},
+        compiler_params=pltpu.CompilerParams(vmem_limit_bytes=VMEM_LIMIT),
         cost_estimate=pl.CostEstimate(flops=2000 * n, bytes_accessed=22 * n, transcendentals=n),
-        name=f"adamw_{which}",
-    )(w, m, v, g, *old)
+        name="adamw",
+    )(*operands, g, *old)
 
 
 def solution(mesh):
@@ -560,13 +692,9 @@
         a0, h1, a1 = forward(x[0], wg, wu, wd)
         g, left, _, _ = backward(a1, a0, h1, dy[0], wg, wu, wd)
         left = lax.psum(left, "dp")
-        new = []
-        for name, which in ((0, 1), (1, 2), (2, 0)):
-            done = (SUMMED - which + 2) // 3
-            first = adamw(which, (0, done), 0, g, w[name], m[name], v[name])
-            new.append((done, which, name, first))
-        out = [adamw(which, (done, 2 * BLOCKS), SUMMED, left, w[name], m[name], v[name], first) for done, which, name, first in new]
-        return tuple(one[kind] for kind in range(3) for one in out)
+        done = adamw((0, SUMMED), 0, g, w, m, v)
+        done = adamw((SUMMED, ALL), SUMMED, left, w, m, v, done)
+        return tuple(done[3 * i + kind] for kind in range(3) for i in range(3))
 
     return jax.shard_map(
         step,

time: 650 us -> 636 us (0.978)
  Pallas kernels: 634 us -> 619 us
    pallas_call x6 -> x2, Pallas kernels: 159 us -> 141 us  [adamw(): pl.pallas_call(functools.partial(adamw_kernel, tuple(rounds), first, len(...]
  transfers between devices with their start and end apart: 1 -> 1, of which waited for: 0 -> 0; matrix products, arithmetic and copies ran while one was open for 0% -> 0% of each run, Pallas kernels for 21% -> 19%
where the time goes in v2:
time: 636 us; the launch traced here: 634 us
  Pallas kernels  619 us (97%)
  between operations  14.1 us (2%)
    pallas_call x1, Pallas kernels, backward(): pl.pallas_call(backward_kernel, out_shape=[jax.ShapeDtypeStruct((SUMMED,...  421 us
    pallas_call x2, Pallas kernels, adamw(): pl.pallas_call(functools.partial(adamw_kernel, tuple(rounds), first, len(...  141 us
    pallas_call x1, Pallas kernels, forward(): pl.pallas_call(functools.partial(forward_kernel, width), grid=(t // tile,...  57 us
  transfers between devices with their start and end apart: 1, of which 0 were waited for; matrix products, arithmetic and copies ran while one was open for 0% of the time, Pallas kernels for 19%

profile of v2, /device:TPU:27, one launch (start us, length us, event | category | flops | bytes accessed | tf_op | source)
XLA Modules:
  0.0 633.6 jit_solution(3636627892503660834)
XLA Ops:
  7.2 0.0 all-reduce.2.cloned.1.call-start
  7.2 57.0 %forward.1 = (bf16[2048,1024]{1,0:T(8,128)(2,1)}, bf16[2048,1024]{1,0:T(8,128)(2,1)}, bf16[2048,1024]{1,0:T(8,128)(2,1)}) custom-call(bf16[2048,1024]{1,0:T(8,128)(2,1)} %bitcast.2, bf16[2,1024,3200]{2,1,0:T(8,128)(2,1)} %refs_0_.3, bf16[2,1024,3200]{2,1,0:T(8,128)(2,1)} %refs_3_.3, bf16[2,3200,1024]{2,1,0:T(8,128)(2,1)} %refs_6_.3), custom_call_target="tpu_custom_call" | custom-call | flops 40265318400 | bytes 36438016 | tf_op jit(solution)/shard_map/forward/pallas_call | solution.py:98
  64.2 421.1 %backward.1 = (bf16[26,640,1024]{2,1,0:T(8,128)(2,1)}, bf16[4,640,1024]{2,1,0:T(8,128)(2,1)}, bf16[26,320,1024]{2,1,0:T(8,128)(2,1)}, bf16[26,320,1024]{2,1,0:T(8,128)(2,1)}) custom-call(bf16[2048,1024]{1,0:T(8,128)(2,1)} %get-tuple-element.32.a1_hbm, bf16[2048,1024]{1,0:T(8,128)(2,1)} %get-tuple-element.33.a0_hbm, ...), custom_call_target="tpu_custom_call" | custom-call | flops 201326592000 | bytes 327680000 | tf_op jit(solution)/shard_map/backward/pallas_call | solution.py:474
  485.3 0.0 all-reduce.2.cloned.1.call-update
  485.3 121.5 %adamw.2 = (bf16[2,1024,3200]{2,1,0:T(8,128)(2,1)}, f32[2,1024,3200]{2,1,0:T(8,128)}, f32[2,1024,3200]{2,1,0:T(8,128)}, bf16[2,1024,3200]{2,1,0:T(8,128)(2,1)}, ...) custom-call(bf16[2,1024,3200]{2,1,0:T(8,128)(2,1)} %refs_0_.3, ...), custom_call_target="tpu_custom_call" | custom-call | flops 34078720000 | bytes 374865920 | tf_op jit(solution)/shard_map/adamw/pallas_call | solution.py:657
  606.8 0.0 all-reduce.2.cloned.1.call-done.refs_9_
  606.9 19.9 %adamw.3 = (bf16[2,1024,3200]{2,1,0:T(8,128)(2,1)}, f32[2,1024,3200]{2,1,0:T(8,128)}, f32[2,1024,3200]{2,1,0:T(8,128)}, bf16[2,1024,3200]{2,1,0:T(8,128)(2,1)}, ...) custom-call(bf16[2,1024,3200]{2,1,0:T(8,128)(2,1)} %refs_0_.3, ...), custom_call_target="tpu_custom_call", output_to_operand_aliasing={{0}: (10, {}), {1}: (11, {}), {2}: (12, {}), {3}: (13, {}),... | custom-call | flops 5242880000 | bytes 57671680 | tf_op jit(solution)/shard_map/adamw/pallas_call | solution.py:657
Async XLA Ops:
  7.2 599.7 %all-reduce.2.cloned.1.call-start = ((), (), s32[]{:S(2)}) async-start(), calls=%async_computation | async-start | bytes 10485760 | tf_op jit(solution)/shard_map/psum | solution.py:694
Sparse Core Ops, SparseCore 0:
  485.4 115.5 all-reduce.1

commit v3 on v2

--- a/solution.py
+++ b/solution.py
@@ -15,7 +15,7 @@
 SUMMED = 26
 UNITS = 5
 FIRST = 8
-SLOTS, SEND_SLOTS, LOAD_SLOTS = 16, 8, 4
+SLOTS, SEND_SLOTS, LOAD_SLOTS = 32, 16, 4
 NN = (((1,), (0,)), ((), ()))
 NT = (((1,), (1,)), ((), ()))
 
@@ -53,13 +53,9 @@
         for i in range(len(pieces)):
             loads(i)[2].start()
 
-    def product(s, n, gate, up):
-        p[:, s : s + n] = (gate * (0.5 * jnp.tanh(0.5 * gate) + 0.5) * up).astype(BF16)
-
     wide = x_ref[...].astype(F32)
     a = (wide * scale_of(wide)).astype(BF16)
     a0_ref[...] = a
-    ready = None
     for i, (s, n) in enumerate(pieces):
 
         @pl.when(first)
@@ -69,20 +65,14 @@
 
         gate = dot(a, wg[:, s : s + n])
         up = dot(a, wu[:, s : s + n])
-        if ready is not None:
-            product(*ready)
-        ready = (s, n, gate, up)
+        p[:, s : s + n] = (gate * (0.5 * jnp.tanh(0.5 * gate) + 0.5) * up).astype(BF16)
 
     @pl.when(first)
     def _():
         for i in range(len(pieces)):
             loads(i)[2].wait()
 
-    last = pieces[-1][0]
-    down = dot(p[:, :last], wd[:last, :])
-    product(*ready)
-    down += dot(p[:, last:], wd[last:, :])
-    h1 = (wide + down.astype(BF16).astype(F32)).astype(BF16)
+    h1 = (wide + dot(p[...], wd[...]).astype(BF16).astype(F32)).astype(BF16)
     h1_ref[...] = h1
     wide1 = h1.astype(F32)
     a1_ref[...] = (wide1 * scale_of(wide1)).astype(BF16)
@@ -114,16 +104,30 @@
     )(x, wg, wu, wd)
 
 
-BLOCK_STEPS, LOW_STEPS = 7, 5
+HALF_STEPS, TILES = 5, 4
+BLOCK_STEPS, LOW_STEPS = 2 * HALF_STEPS + TILES, 2 * HALF_STEPS
 TURN = BLOCKS * BLOCK_STEPS
-STEPS = TURN + 1 + BLOCKS * LOW_STEPS
+STEPS = TURN + TILES + BLOCKS * LOW_STEPS
 
 
 def step_of(s):
-    low = s - (TURN + 1)
-    block = jnp.where(s < TURN, s // BLOCK_STEPS, jnp.where(s == TURN, BLOCKS, BLOCKS + low // LOW_STEPS))
-    kind = jnp.where(s < TURN, s % BLOCK_STEPS, jnp.where(s == TURN, 7, low % LOW_STEPS))
-    return block, kind
+    low = s - (TURN + TILES)
+    block = jnp.where(s < TURN, s // BLOCK_STEPS, jnp.where(low < 0, BLOCKS, BLOCKS + low // LOW_STEPS))
+    place = jnp.where(s < TURN, s % BLOCK_STEPS, jnp.where(low < 0, BLOCK_STEPS + s - TURN, low % LOW_STEPS))
+    return block, place
+
+
+def summed_piece(c):
+    full, rest = SUMMED // 3, max(SUMMED % 3, 1)
+    late = c - 6 * full
+    return tuple(
+        jnp.where(late < 0, early, other) for early, other in ((c // 6, full), (c % 6 // 3, late // rest), (c % 3, late % rest))
+    )
+
+
+def place_of(block, half, which):
+    full, rest = SUMMED // 3, SUMMED % 3
+    return jnp.where(block < full, 6 * block + 3 * half + which, 6 * full + rest * half + which)
 
 
 def backward_kernel(
@@ -136,9 +140,9 @@
     z, core = me // 2, me % 2
     partner = me + 1 - 2 * core
     t, d = ad.shape[1:]
-    f = stage.shape[1]
-    half, r = f // 2, f // 2 // UNITS
-    units = SUMMED * UNITS
+    f, fs = wgt.shape[0], stage.shape[1]
+    part, r = fs // 2, fs // 2 // UNITS
+    units = 2 * SUMMED * UNITS
     sub = dat.shape[2]
 
     def remote(src, dst, send, recv, device):
@@ -177,15 +181,18 @@
 
     pl.semaphore_wait(barrier, 3 - z // 3 - (3 - z) // 3)
 
-    def hidden(block, kind):
+    def at_half(half):
+        return pl.ds(pl.multiple_of(half * fs, fs), fs)
+
+    def hidden(block, half, tokens):
         slot = block % 2
 
-        @pl.when(kind == 0)
+        @pl.when((half == 0) & (tokens == 0))
         def _():
             @pl.when(block == 0)
             def _():
+                load_a1.wait()
                 load_dy.wait()
-                load_a1.wait()
 
             @pl.when(block == BLOCKS)
             def _():
@@ -202,92 +209,89 @@
             wgt[...] = wgb[slot].T
             wut[...] = wub[slot].T
 
+        units_at = at_half(half)
         for i in range(t // 2 // sub):
-            at = pl.ds(pl.multiple_of(kind * (t // 2) + i * sub, sub), sub)
-            gate = dot(wgt[...], ad[1, at, :], NT)
-            up = dot(wut[...], ad[1, at, :], NT)
-            dp = dot(wdb[slot], ad[0, at, :], NT).astype(BF16).astype(F32)
+            at = pl.ds(pl.multiple_of(tokens * (t // 2) + i * sub, sub), sub)
+            gate = dot(wgt[units_at, :], ad[1, at, :], NT)
+            up = dot(wut[units_at, :], ad[1, at, :], NT)
+            dp = dot(wdb[slot, units_at, :], ad[0, at, :], NT).astype(BF16).astype(F32)
             sig = 0.5 * jnp.tanh(0.5 * gate) + 0.5
             silu = gate * sig
-            pgu[0, :, at] = (silu * up).astype(BF16)
-            pgu[1, :, at] = (dp * up * (sig + silu * (1.0 - sig))).astype(BF16)
-            pgu[2, :, at] = (dp * silu).astype(BF16)
-
-    def gradient(block, kind):
-        which = kind - 2
-        slot = (3 * block + which) % 2
+            pgu[0, units_at, at] = (silu * up).astype(BF16)
+            pgu[1, units_at, at] = (dp * up * (sig + silu * (1.0 - sig))).astype(BF16)
+            pgu[2, units_at, at] = (dp * silu).astype(BF16)
+
+    def gradient(block, half, which):
         rhs = jnp.minimum(which, 1)
-        lhs = pgu[which]
-        for i in range(2):
-            cols = slice(i * (d // 2), (i + 1) * (d // 2))
-            stage[slot, :, cols] = dot(lhs, ad[rhs, :, cols]).astype(BF16)
-
-    def to_input(block, kind):
+        stage[slot_of(half, which)] = dot(pgu[which, at_half(half), :], ad[rhs]).astype(BF16)
+
+    def to_input(block, tile):
         slot = block % 2
 
-        @pl.when((block == BLOCKS - 1) & (kind == 5))
+        @pl.when((block == BLOCKS - 1) & (tile == 0))
         def _():
             load_h1.start()
 
-        for i in range(t // 2 // sub):
-            tile = (kind - 5) * (t // 2 // sub) + i
-            at = pl.ds(pl.multiple_of(tile * sub, sub), sub)
-            dat[tile] += dot(wgb[slot], pgu[1, :, at]) + dot(wub[slot], pgu[2, :, at])
-
-    def turn():
-        load_h1.wait()
-
-        def body(i, _):
-            at = pl.ds(pl.multiple_of(i * sub, sub), sub)
-            da = dat[i].T.astype(BF16).astype(F32)
-            wide = ad[1, at, :].astype(F32)
-            scale = scale_of(wide)
-            inner = jnp.sum(da * wide, -1, keepdims=True) * (scale * scale * scale) * (1.0 / d)
-            through = (da * scale - wide * inner).astype(BF16).astype(F32)
-            ad[0, at, :] = (ad[0, at, :].astype(F32) + through).astype(BF16)
-            return 0
-
-        lax.fori_loop(0, t // sub, body, 0)
-        load_a0.start()
+        at = pl.ds(pl.multiple_of(tile * sub, sub), sub)
+        dat[tile] += dot(wgb[slot], pgu[1, :, at]) + dot(wub[slot], pgu[2, :, at])
+
+    def turn(tile):
+        @pl.when(tile == 0)
+        def _():
+            load_h1.wait()
+
+        at = pl.ds(pl.multiple_of(tile * sub, sub), sub)
+        da = dat[tile].T.astype(BF16).astype(F32)
+        wide = ad[1, at, :].astype(F32)
+        scale = scale_of(wide)
+        inner = jnp.sum(da * wide, -1, keepdims=True) * (scale * scale * scale) * (1.0 / d)
+        through = (da * scale - wide * inner).astype(BF16).astype(F32)
+        ad[0, at, :] = (ad[0, at, :].astype(F32) + through).astype(BF16)
+
+        @pl.when(tile == TILES - 1)
+        def _():
+            load_a0.start()
+
+    def slot_of(half, which):
+        return (half + which) % 2
 
     def rows(slot, c):
-        return stage.at[slot, pl.ds(pl.multiple_of(c * half, half), half), :]
-
-    def piece_copies(q):
-        slot = q % 2
-        own = pltpu.make_async_copy(rows(slot, core), mine_hbm.at[q], own_sem.at[q])
-        give = remote(rows(slot, 1 - core), theirs_hbm.at[q], give_sem.at[slot], get_sem.at[q], partner)
-        return own, give
-
-    def left_copy(q):
-        return pltpu.make_async_copy(stage.at[q % 2], left_hbm.at[q - SUMMED], left_sem.at[q % 2])
-
-    def send_stage(q):
-        @pl.when(q < SUMMED)
-        def _():
-            own, give = piece_copies(q)
-            own.start()
-            give.start()
-
-        @pl.when(q >= SUMMED)
-        def _():
-            left_copy(q).start()
-
-    def wait_stage(q):
-        @pl.when(q < SUMMED)
-        def _():
-            own, give = piece_copies(q)
-            own.wait()
-            give.wait_send()
-
-        @pl.when(q >= SUMMED)
-        def _():
-            left_copy(q).wait()
+        return stage.at[slot, pl.ds(pl.multiple_of(c * part, part), part), :]
+
+    def give_copy(slot, c):
+        return remote(rows(slot, 1 - core), theirs_hbm.at[c], give_sem.at[slot], get_sem.at[c], partner)
+
+    def own_copy(slot, c):
+        return pltpu.make_async_copy(rows(slot, core), mine_hbm.at[c], own_sem.at[slot])
+
+    def left_copy(slot, block, half, which):
+        return pltpu.make_async_copy(stage.at[slot], left_hbm.at[3 * block + which - SUMMED, at_half(half), :], left_sem.at[slot])
+
+    def stage_copies(block, half, which, go):
+        slot, here = slot_of(half, which), 3 * block + which < SUMMED
+
+        @pl.when(here)
+        def _():
+            c = place_of(block, half, which)
+            if go:
+                own_copy(slot, c).start()
+                give_copy(slot, c).start()
+            else:
+                own_copy(slot, c).wait()
+                give_copy(slot, c).wait_send()
+
+        @pl.when(jnp.logical_not(here))
+        def _():
+            copy = left_copy(slot, block, half, which)
+            if go:
+                copy.start()
+            else:
+                copy.wait()
 
     is0, is1, is2, is3 = z == 0, z == 1, z == 2, z == 3
-    sum_lag = jnp.where(is1, 4, jnp.where(is2, 2, 0))
-    tot_lag = jnp.where(is1, 4, jnp.where(is3, 10, 7))
-    free_lag = tot_lag + jnp.where(is3, 3, 4)
+    sum_lag = jnp.where(is1, 6, jnp.where(is2, 3, 0))
+    tot_lag = jnp.where(is1, 6, jnp.where(is3, 15, 11))
+    free_lag = tot_lag + jnp.where(is3, 4, 6)
 
     def load_copies(k):
         q, at, slot = k // UNITS, pl.ds(pl.multiple_of((k % UNITS) * r, r), r), k % LOAD_SLOTS
@@ -309,7 +313,8 @@
         return remote(tot.at[k % SLOTS], tot.at[k % SLOTS], up_sem.at[k % SLOTS], tot_sem.at[k % SLOTS], me + 2)
 
     def out_copies(k):
-        q, at, slot = k // UNITS, pl.ds(pl.multiple_of(core * half + (k % UNITS) * r, r), r), k % SLOTS
+        block, half, which = summed_piece(k // UNITS)
+        q, at, slot = 3 * block + which, pl.ds(pl.multiple_of(half * fs + core * part + (k % UNITS) * r, r), r), k % SLOTS
         return (
             pltpu.make_async_copy(tot.at[slot], g_hbm.at[q, at, :], keep_sem.at[slot]),
             remote(tot.at[slot], g_hbm.at[q, at, :], pass_sem.at[slot], partner_sem, partner),
@@ -396,7 +401,7 @@
         def _():
             @pl.when(k % UNITS == 0)
             def _():
-                piece_copies(k // UNITS)[1].wait_recv()
+                give_copy(0, k // UNITS).wait_recv()
 
             for c in load_copies(k):
                 c.start()
@@ -408,16 +413,17 @@
 
         @pl.when((step >= 1) & (step <= STEPS))
         def _():
-            block, kind = step_of(step - 1)
-            q = 3 * block + kind - 2
-
-            @pl.when((kind >= 2) & (kind <= 4) & works)
-            def _():
-                send_stage(q)
-
-            @pl.when((kind >= 2) & (kind <= 4) & (i % 2 == 1))
-            def _():
-                wait_stage(q)
+            block, place = step_of(step - 1)
+            half, kind = place // HALF_STEPS, place % HALF_STEPS
+            made = (place < LOW_STEPS) & (kind >= 2)
+
+            @pl.when(made & works)
+            def _():
+                stage_copies(block, half, kind - 2, True)
+
+            @pl.when(made & (i % 2 == 1))
+            def _():
+                stage_copies(block, half, kind - 2, False)
 
         now = i - FIRST
         free(now - free_lag)
@@ -428,27 +434,28 @@
 
         @pl.when(works & (step < STEPS))
         def _():
-            block, kind = step_of(step)
-
-            @pl.when(kind <= 1)
-            def _():
-                hidden(block, kind)
-
-            @pl.when((kind >= 2) & (kind <= 4))
-            def _():
-                gradient(block, kind)
-
-            @pl.when((kind == 5) | (kind == 6))
-            def _():
-                to_input(block, kind)
-
-            @pl.when(kind == 7)
-            def _():
-                turn()
+            block, place = step_of(step)
+            half, kind = place // HALF_STEPS, place % HALF_STEPS
+
+            @pl.when((place < LOW_STEPS) & (kind < 2))
+            def _():
+                hidden(block, half, kind)
+
+            @pl.when((place < LOW_STEPS) & (kind >= 2))
+            def _():
+                gradient(block, half, kind - 2)
+
+            @pl.when((place >= LOW_STEPS) & (place < BLOCK_STEPS))
+            def _():
+                to_input(block, place - LOW_STEPS)
+
+            @pl.when(place >= BLOCK_STEPS)
+            def _():
+                turn(place - BLOCK_STEPS)
 
         return 0
 
-    lax.fori_loop(0, max(FIRST + units + 14, 2 * STEPS + 2), tick, 0)
+    lax.fori_loop(0, max(FIRST + units + 20, 2 * STEPS + 2), tick, 0)
 
     for k in range(units - SEND_SLOTS, units):
 
@@ -467,8 +474,9 @@
     t, d = a1.shape
     ff = wg.shape[2]
     f = ff // BLOCKS
-    r = f // 2 // UNITS
-    sub = t // 4
+    fs = f // 2
+    r = fs // 2 // UNITS
+    sub = t // TILES
     anywhere = pl.BlockSpec(memory_space=pl.ANY)
     dma = pltpu.SemaphoreType.DMA
     return pl.pallas_call(
@@ -476,8 +484,8 @@
         out_shape=[
             jax.ShapeDtypeStruct((SUMMED, f, d), BF16),
             jax.ShapeDtypeStruct((ALL - SUMMED, f, d), BF16),
-            jax.ShapeDtypeStruct((SUMMED, f // 2, d), BF16),
-            jax.ShapeDtypeStruct((SUMMED, f // 2, d), BF16),
+            jax.ShapeDtypeStruct((2 * SUMMED, fs // 2, d), BF16),
+            jax.ShapeDtypeStruct((2 * SUMMED, fs // 2, d), BF16),
         ],
         in_specs=[anywhere] * 7,
         out_specs=[anywhere] * 4,
@@ -489,8 +497,8 @@
             pltpu.VMEM((2, f, d), BF16),
             pltpu.VMEM((f, d), BF16),
             pltpu.VMEM((f, d), BF16),
-            pltpu.VMEM((4, d, sub), F32),
-            pltpu.VMEM((2, f, d), BF16),
+            pltpu.VMEM((TILES, d, sub), F32),
+            pltpu.VMEM((2, fs, d), BF16),
             pltpu.VMEM((LOAD_SLOTS, r, d), BF16),
             pltpu.VMEM((LOAD_SLOTS, r, d), BF16),
             pltpu.VMEM((SEND_SLOTS, r, d), BF16),
@@ -499,9 +507,9 @@
             pltpu.VMEM((SLOTS, r, d), BF16),
             dma((4,)),
             dma((2, 3)),
-            dma((SUMMED,)),
             dma((2,)),
-            dma((SUMMED,)),
+            dma((2,)),
+            dma((2 * SUMMED,)),
             dma((2,)),
             dma((LOAD_SLOTS, 2)),
             dma((SEND_SLOTS,)),

time: 636 us -> 674 us (1.060)
  Pallas kernels: 619 us -> 651 us
    pallas_call x1, Pallas kernels: 421 us -> 457 us  [backward(): pl.pallas_call(backward_kernel, out_shape=[jax.ShapeDtypeStruct((SUMMED,...]
  transfers between devices with their start and end apart: 1 -> 1, of which waited for: 0 -> 0; matrix products, arithmetic and copies ran while one was open for 0% -> 0% of each run, Pallas kernels for 19% -> 18%
where the time goes in v3:
time: 674 us; the launch traced here: 665 us
  Pallas kernels  651 us (97%)
  between operations  14.1 us (2%)
    pallas_call x1, Pallas kernels, backward(): pl.pallas_call(backward_kernel, out_shape=[jax.ShapeDtypeStruct((SUMMED,...  457 us
    pallas_call x2, Pallas kernels, adamw(): pl.pallas_call(functools.partial(adamw_kernel, tuple(rounds), first, len(...  141 us
    pallas_call x1, Pallas kernels, forward(): pl.pallas_call(functools.partial(forward_kernel, width), grid=(t // tile,...  52.3 us
  transfers between devices with their start and end apart: 1, of which 0 were waited for; matrix products, arithmetic and copies ran while one was open for 0% of the time, Pallas kernels for 18%

profile of v3, /device:TPU:27, one launch (start us, length us, event | category | flops | bytes accessed | tf_op | source)
XLA Modules:
  0.0 665.1 jit_solution(12712613327339327931)
XLA Ops:
  7.2 0.0 all-reduce.2.cloned.1.call-start
  7.2 52.3 %forward.1 = (bf16[2048,1024]{1,0:T(8,128)(2,1)}, bf16[2048,1024]{1,0:T(8,128)(2,1)}, bf16[2048,1024]{1,0:T(8,128)(2,1)}) custom-call(bf16[2048,1024]{1,0:T(8,128)(2,1)} %bitcast.2, bf16[2,1024,3200]{2,1,0:T(8,128)(2,1)} %refs_0_.3, bf16[2,1024,3200]{2,1,0:T(8,128)(2,1)} %refs_3_.3, bf16[2,3200,1024]{2,1,0:T(8,128)(2,1)} %refs_6_.3), custom_call_target="tpu_custom_call" | custom-call | flops 40265318400 | bytes 36438016 | tf_op jit(solution)/shard_map/forward/pallas_call | solution.py:88
  59.6 457.2 %backward.1 = (bf16[26,640,1024]{2,1,0:T(8,128)(2,1)}, bf16[4,640,1024]{2,1,0:T(8,128)(2,1)}, bf16[52,160,1024]{2,1,0:T(8,128)(2,1)}, bf16[52,160,1024]{2,1,0:T(8,128)(2,1)}) custom-call(bf16[2048,1024]{1,0:T(8,128)(2,1)} %get-tuple-element.32.a1_hbm, bf16[2048,1024]{1,0:T(8,128)(2,1)} %get-tuple-element.33.a0_hbm, ...), custom_call_target="tpu_custom_call" | custom-call | flops 201326592000 | bytes 327680000 | tf_op jit(solution)/shard_map/backward/pallas_call | solution.py:482
  516.8 0.0 all-reduce.2.cloned.1.call-update
  516.8 121.5 %adamw.2 = (bf16[2,1024,3200]{2,1,0:T(8,128)(2,1)}, f32[2,1024,3200]{2,1,0:T(8,128)}, f32[2,1024,3200]{2,1,0:T(8,128)}, bf16[2,1024,3200]{2,1,0:T(8,128)(2,1)}, ...) custom-call(bf16[2,1024,3200]{2,1,0:T(8,128)(2,1)} %refs_0_.3, ...), custom_call_target="tpu_custom_call" | custom-call | flops 34078720000 | bytes 374865920 | tf_op jit(solution)/shard_map/adamw/pallas_call | solution.py:665
  638.3 0.0 all-reduce.2.cloned.1.call-done.refs_9_
  638.3 19.9 %adamw.3 = (bf16[2,1024,3200]{2,1,0:T(8,128)(2,1)}, f32[2,1024,3200]{2,1,0:T(8,128)}, f32[2,1024,3200]{2,1,0:T(8,128)}, bf16[2,1024,3200]{2,1,0:T(8,128)(2,1)}, ...) custom-call(bf16[2,1024,3200]{2,1,0:T(8,128)(2,1)} %refs_0_.3, ...), custom_call_target="tpu_custom_call", output_to_operand_aliasing={{0}: (10, {}), {1}: (11, {}), {2}: (12, {}), {3}: (13, {}),... | custom-call | flops 5242880000 | bytes 57671680 | tf_op jit(solution)/shard_map/adamw/pallas_call | solution.py:665
Async XLA Ops:
  7.2 631.1 %all-reduce.2.cloned.1.call-start = ((), (), s32[]{:S(2)}) async-start(), calls=%async_computation | async-start | bytes 10485760 | tf_op jit(solution)/shard_map/psum | solution.py:702
Sparse Core Ops, SparseCore 0:
  516.9 115.5 all-reduce.1

commit v4 on v3

--- a/solution.py
+++ b/solution.py
@@ -13,9 +13,9 @@
 BLOCKS = 5
 ALL = 6 * BLOCKS
 SUMMED = 26
-UNITS = 5
-FIRST = 8
-SLOTS, SEND_SLOTS, LOAD_SLOTS = 32, 16, 4
+UNITS = 2
+FIRST = 4
+SLOTS, SEND_SLOTS, LOAD_SLOTS = 12, 6, 4
 NN = (((1,), (0,)), ((), ()))
 NT = (((1,), (1,)), ((), ()))
 
@@ -104,14 +104,14 @@
     )(x, wg, wu, wd)
 
 
-HALF_STEPS, TILES = 5, 4
-BLOCK_STEPS, LOW_STEPS = 2 * HALF_STEPS + TILES, 2 * HALF_STEPS
+HALF_STEPS, DA_STEPS, TILES = 4, 2, 4
+BLOCK_STEPS, LOW_STEPS = 2 * HALF_STEPS + DA_STEPS, 2 * HALF_STEPS
 TURN = BLOCKS * BLOCK_STEPS
-STEPS = TURN + TILES + BLOCKS * LOW_STEPS
+STEPS = TURN + DA_STEPS + BLOCKS * LOW_STEPS
 
 
 def step_of(s):
-    low = s - (TURN + TILES)
+    low = s - (TURN + DA_STEPS)
     block = jnp.where(s < TURN, s // BLOCK_STEPS, jnp.where(low < 0, BLOCKS, BLOCKS + low // LOW_STEPS))
     place = jnp.where(s < TURN, s % BLOCK_STEPS, jnp.where(low < 0, BLOCK_STEPS + s - TURN, low % LOW_STEPS))
     return block, place
@@ -184,10 +184,10 @@
     def at_half(half):
         return pl.ds(pl.multiple_of(half * fs, fs), fs)
 
-    def hidden(block, half, tokens):
+    def hidden(block, half):
         slot = block % 2
 
-        @pl.when((half == 0) & (tokens == 0))
+        @pl.when(half == 0)
         def _():
             @pl.when(block == 0)
             def _():
@@ -210,8 +210,8 @@
             wut[...] = wub[slot].T
 
         units_at = at_half(half)
-        for i in range(t // 2 // sub):
-            at = pl.ds(pl.multiple_of(tokens * (t // 2) + i * sub, sub), sub)
+        for i in range(TILES):
+            at = pl.ds(i * sub, sub)
             gate = dot(wgt[units_at, :], ad[1, at, :], NT)
             up = dot(wut[units_at, :], ad[1, at, :], NT)
             dp = dot(wdb[slot, units_at, :], ad[0, at, :], NT).astype(BF16).astype(F32)
@@ -225,30 +225,37 @@
         rhs = jnp.minimum(which, 1)
         stage[slot_of(half, which)] = dot(pgu[which, at_half(half), :], ad[rhs]).astype(BF16)
 
-    def to_input(block, tile):
+    def to_input(block, step):
         slot = block % 2
 
-        @pl.when((block == BLOCKS - 1) & (tile == 0))
+        @pl.when((block == BLOCKS - 1) & (step == 0))
         def _():
             load_h1.start()
 
-        at = pl.ds(pl.multiple_of(tile * sub, sub), sub)
-        dat[tile] += dot(wgb[slot], pgu[1, :, at]) + dot(wub[slot], pgu[2, :, at])
-
-    def turn(tile):
-        @pl.when(tile == 0)
+        for i in range(TILES // DA_STEPS):
+            tile = step * (TILES // DA_STEPS) + i
+            at = pl.ds(pl.multiple_of(tile * sub, sub), sub)
+            dat[tile] += dot(wgb[slot], pgu[1, :, at]) + dot(wub[slot], pgu[2, :, at])
+
+    def turn(step):
+        @pl.when(step == 0)
         def _():
             load_h1.wait()
 
-        at = pl.ds(pl.multiple_of(tile * sub, sub), sub)
-        da = dat[tile].T.astype(BF16).astype(F32)
-        wide = ad[1, at, :].astype(F32)
-        scale = scale_of(wide)
-        inner = jnp.sum(da * wide, -1, keepdims=True) * (scale * scale * scale) * (1.0 / d)
-        through = (da * scale - wide * inner).astype(BF16).astype(F32)
-        ad[0, at, :] = (ad[0, at, :].astype(F32) + through).astype(BF16)
-
-        @pl.when(tile == TILES - 1)
+        def body(i, _):
+            tile = step * (TILES // DA_STEPS) + i
+            at = pl.ds(pl.multiple_of(tile * sub, sub), sub)
+            da = dat[tile].T.astype(BF16).astype(F32)
+            wide = ad[1, at, :].astype(F32)
+            scale = scale_of(wide)
+            inner = jnp.sum(da * wide, -1, keepdims=True) * (scale * scale * scale) * (1.0 / d)
+            through = (da * scale - wide * inner).astype(BF16).astype(F32)
+            ad[0, at, :] = (ad[0, at, :].astype(F32) + through).astype(BF16)
+            return 0
+
+        lax.fori_loop(0, TILES // DA_STEPS, body, 0)
+
+        @pl.when(step == DA_STEPS - 1)
         def _():
             load_a0.start()
 
@@ -289,9 +296,9 @@
                 copy.wait()
 
     is0, is1, is2, is3 = z == 0, z == 1, z == 2, z == 3
-    sum_lag = jnp.where(is1, 6, jnp.where(is2, 3, 0))
-    tot_lag = jnp.where(is1, 6, jnp.where(is3, 15, 11))
-    free_lag = tot_lag + jnp.where(is3, 4, 6)
+    sum_lag = jnp.where(is1, 2, jnp.where(is2, 1, 0))
+    tot_lag = jnp.where(is1, 2, jnp.where(is3, 9, 6))
+    free_lag = tot_lag + jnp.where(is3, 2, 3)
 
     def load_copies(k):
         q, at, slot = k // UNITS, pl.ds(pl.multiple_of((k % UNITS) * r, r), r), k % LOAD_SLOTS
@@ -407,24 +414,19 @@
                 c.start()
 
 
+    def stage_of(s, go):
+        @pl.when((s >= 0) & (s < STEPS))
+        def _():
+            block, place = step_of(s)
+            half, kind = place // HALF_STEPS, place % HALF_STEPS
+
+            @pl.when((place < LOW_STEPS) & (kind >= 1))
+            def _():
+                stage_copies(block, half, kind - 1, go)
+
     def tick(i, _):
-        step = i // 2
-        works = i % 2 == 0
-
-        @pl.when((step >= 1) & (step <= STEPS))
-        def _():
-            block, place = step_of(step - 1)
-            half, kind = place // HALF_STEPS, place % HALF_STEPS
-            made = (place < LOW_STEPS) & (kind >= 2)
-
-            @pl.when(made & works)
-            def _():
-                stage_copies(block, half, kind - 2, True)
-
-            @pl.when(made & (i % 2 == 1))
-            def _():
-                stage_copies(block, half, kind - 2, False)
-
+        stage_of(i - 2, False)
+        stage_of(i - 1, True)
         now = i - FIRST
         free(now - free_lag)
         add(now - sum_lag)
@@ -432,18 +434,18 @@
         send(now - sum_lag, now - tot_lag)
         load(now - sum_lag + 1)
 
-        @pl.when(works & (step < STEPS))
-        def _():
-            block, place = step_of(step)
+        @pl.when(i < STEPS)
+        def _():
+            block, place = step_of(i)
             half, kind = place // HALF_STEPS, place % HALF_STEPS
 
-            @pl.when((place < LOW_STEPS) & (kind < 2))
-            def _():
-                hidden(block, half, kind)
-
-            @pl.when((place < LOW_STEPS) & (kind >= 2))
-            def _():
-                gradient(block, half, kind - 2)
+            @pl.when((place < LOW_STEPS) & (kind == 0))
+            def _():
+                hidden(block, half)
+
+            @pl.when((place < LOW_STEPS) & (kind >= 1))
+            def _():
+                gradient(block, half, kind - 1)
 
             @pl.when((place >= LOW_STEPS) & (place < BLOCK_STEPS))
             def _():
@@ -455,7 +457,7 @@
 
         return 0
 
-    lax.fori_loop(0, max(FIRST + units + 20, 2 * STEPS + 2), tick, 0)
+    lax.fori_loop(0, max(FIRST + units + 12, STEPS + 2), tick, 0)
 
     for k in range(units - SEND_SLOTS, units):
 

time: 674 us -> 624 us (0.926); the launches traced: 665 us -> 624 us
  Pallas kernels: 651 us -> 609 us
    pallas_call x1, Pallas kernels: 457 us -> 416 us  [backward(): pl.pallas_call(backward_kernel, out_shape=[jax.ShapeDtypeStruct((SUMMED,...]
  transfers between devices with their start and end apart: 1 -> 1, of which waited for: 0 -> 0; matrix products, arithmetic and copies ran while one was open for 0% -> 0% of each run, Pallas kernels for 18% -> 19%
where the time goes in v4:
time: 624 us
  Pallas kernels  609 us (98%)
  between operations  14.1 us (2%)
    pallas_call x1, Pallas kernels, backward(): pl.pallas_call(backward_kernel, out_shape=[jax.ShapeDtypeStruct((SUMMED,...  416 us
    pallas_call x2, Pallas kernels, adamw(): pl.pallas_call(functools.partial(adamw_kernel, tuple(rounds), first, len(...  141 us
    pallas_call x1, Pallas kernels, forward(): pl.pallas_call(functools.partial(forward_kernel, width), grid=(t // tile,...  52.3 us
  transfers between devices with their start and end apart: 1, of which 0 were waited for; matrix products, arithmetic and copies ran while one was open for 0% of the time, Pallas kernels for 19%

profile of v4, /device:TPU:27, one launch (start us, length us, event | category | flops | bytes accessed | tf_op | source)
XLA Modules:
  0.0 623.5 jit_solution(5476470875901694218)
XLA Ops:
  7.2 0.0 all-reduce.2.cloned.1.call-start
  7.2 52.3 %forward.1 = (bf16[2048,1024]{1,0:T(8,128)(2,1)}, bf16[2048,1024]{1,0:T(8,128)(2,1)}, bf16[2048,1024]{1,0:T(8,128)(2,1)}) custom-call(bf16[2048,1024]{1,0:T(8,128)(2,1)} %bitcast.2, bf16[2,1024,3200]{2,1,0:T(8,128)(2,1)} %refs_0_.3, bf16[2,1024,3200]{2,1,0:T(8,128)(2,1)} %refs_3_.3, bf16[2,3200,1024]{2,1,0:T(8,128)(2,1)} %refs_6_.3), custom_call_target="tpu_custom_call" | custom-call | flops 40265318400 | bytes 36438016 | tf_op jit(solution)/shard_map/forward/pallas_call | solution.py:88
  59.6 415.6 %backward.1 = (bf16[26,640,1024]{2,1,0:T(8,128)(2,1)}, bf16[4,640,1024]{2,1,0:T(8,128)(2,1)}, bf16[52,160,1024]{2,1,0:T(8,128)(2,1)}, bf16[52,160,1024]{2,1,0:T(8,128)(2,1)}) custom-call(bf16[2048,1024]{1,0:T(8,128)(2,1)} %get-tuple-element.32.a1_hbm, bf16[2048,1024]{1,0:T(8,128)(2,1)} %get-tuple-element.33.a0_hbm, ...), custom_call_target="tpu_custom_call" | custom-call | flops 201326592000 | bytes 327680000 | tf_op jit(solution)/shard_map/backward/pallas_call | solution.py:484
  475.2 0.0 all-reduce.2.cloned.1.call-update
  475.2 121.5 %adamw.2 = (bf16[2,1024,3200]{2,1,0:T(8,128)(2,1)}, f32[2,1024,3200]{2,1,0:T(8,128)}, f32[2,1024,3200]{2,1,0:T(8,128)}, bf16[2,1024,3200]{2,1,0:T(8,128)(2,1)}, ...) custom-call(bf16[2,1024,3200]{2,1,0:T(8,128)(2,1)} %refs_0_.3, ...), custom_call_target="tpu_custom_call" | custom-call | flops 34078720000 | bytes 374865920 | tf_op jit(solution)/shard_map/adamw/pallas_call | solution.py:667
  596.7 0.0 all-reduce.2.cloned.1.call-done.refs_9_
  596.8 19.9 %adamw.3 = (bf16[2,1024,3200]{2,1,0:T(8,128)(2,1)}, f32[2,1024,3200]{2,1,0:T(8,128)}, f32[2,1024,3200]{2,1,0:T(8,128)}, bf16[2,1024,3200]{2,1,0:T(8,128)(2,1)}, ...) custom-call(bf16[2,1024,3200]{2,1,0:T(8,128)(2,1)} %refs_0_.3, ...), custom_call_target="tpu_custom_call", output_to_operand_aliasing={{0}: (10, {}), {1}: (11, {}), {2}: (12, {}), {3}: (13, {}),... | custom-call | flops 5242880000 | bytes 57671680 | tf_op jit(solution)/shard_map/adamw/pallas_call | solution.py:667
Async XLA Ops:
  7.2 589.6 %all-reduce.2.cloned.1.call-start = ((), (), s32[]{:S(2)}) async-start(), calls=%async_computation | async-start | bytes 10485760 | tf_op jit(solution)/shard_map/psum | solution.py:704
Sparse Core Ops, SparseCore 0:
  475.3 115.5 all-reduce.1

commit v5 on v4

--- a/solution.py
+++ b/solution.py
@@ -14,6 +14,7 @@
 ALL = 6 * BLOCKS
 SUMMED = 26
 UNITS = 2
+FINE, PIECES = 2, 5
 FIRST = 4
 SLOTS, SEND_SLOTS, LOAD_SLOTS = 12, 6, 4
 NN = (((1,), (0,)), ((), ()))
@@ -81,7 +82,7 @@
 def forward(x, wg, wu, wd):
     t, d = x.shape
     ff = wg.shape[2]
-    tile = min(t, 512)
+    tile = min(t, 1024)
     width = min(ff, 768)
     rows = pl.BlockSpec((tile, d), lambda i: (i, 0))
     anywhere = pl.BlockSpec(memory_space=pl.ANY)
@@ -133,8 +134,9 @@
 def backward_kernel(
     a1_hbm, a0_hbm, h1_hbm, dy_hbm, wg_hbm, wu_hbm, wd_hbm,
     g_hbm, left_hbm, mine_hbm, theirs_hbm,
-    ad, pgu, wgb, wub, wdb, wgt, wut, dat, stage, mb, xb, sb, ra, rb, tot,
+    ad, pgu, wgb, wub, wdb, wgt, wut, dat, stage, mb, xb, sb, ra, rb, tot, fsb, fra, frb, ftot,
     in_sem, w_sem, own_sem, give_sem, get_sem, left_sem, load_sem, s_sem, ra_sem, rb_sem, tot_sem, down_sem, up_sem, keep_sem, pass_sem, partner_sem,
+    fs_sem, fra_sem, frb_sem, ftot_sem, fdown_sem, fup_sem, fkeep_sem, fpass_sem,
 ):
     me = lax.axis_index("dp")
     z, core = me // 2, me % 2
@@ -143,6 +145,7 @@
     f, fs = wgt.shape[0], stage.shape[1]
     part, r = fs // 2, fs // 2 // UNITS
     units = 2 * SUMMED * UNITS
+    coarse = units - FINE
     sub = dat.shape[2]
 
     def remote(src, dst, send, recv, device):
@@ -328,7 +331,7 @@
         )
 
     def inside(k):
-        return (k >= 0) & (k < units)
+        return (k >= 0) & (k < coarse)
 
     def free(k):
         @pl.when(inside(k))
@@ -403,8 +406,115 @@
             for c in out_copies(k_tot):
                 c.start()
 
+    def fine_edge(j):
+        return remote(fsb.at[j], fra.at[j], fs_sem.at[j], fra_sem.at[j], me + 2 - 4 * (z // 3))
+
+    def fine_inner(j):
+        return remote(fsb.at[j], frb.at[j], fs_sem.at[j], frb_sem.at[j], me - 2)
+
+    def fine_down(j):
+        return remote(ftot.at[j], ftot.at[j], fdown_sem.at[j], ftot_sem.at[j], me - 2)
+
+    def fine_up(j):
+        return remote(ftot.at[j], ftot.at[j], fup_sem.at[j], ftot_sem.at[j], me + 2)
+
+    def fine_out(j):
+        fr = r // PIECES
+        k = coarse + j // PIECES
+        block, half, which = summed_piece(k // UNITS)
+        row = half * fs + core * part + (k % UNITS) * r + (j % PIECES) * fr
+        q, at = 3 * block + which, pl.ds(pl.multiple_of(row, fr), fr)
+        return (
+            pltpu.make_async_copy(ftot.at[j], g_hbm.at[q, at, :], fkeep_sem.at[j]),
+            remote(ftot.at[j], g_hbm.at[q, at, :], fpass_sem.at[j], partner_sem, partner),
+        )
+
+    def fine_send(j):
+        @pl.when(is1)
+        def _():
+            fine_up(j).start()
+            fine_down(j).start()
+
+        @pl.when(is2)
+        def _():
+            fine_up(j).start()
+
+        for c in fine_out(j):
+            c.start()
+
+    def fine_add(k):
+        @pl.when((k >= coarse) & (k < units))
+        def _():
+            for c in load_copies(k):
+                c.wait()
+            fr, slot = r // PIECES, k % LOAD_SLOTS
+
+            def body(i, _):
+                j = (k - coarse) * PIECES + i
+                at = pl.ds(pl.multiple_of(i * fr, fr), fr)
+                both = mb[slot, at, :].astype(F32) + xb[slot, at, :].astype(F32)
+
+                @pl.when(is0 | is3)
+                def _():
+                    fsb[j] = both.astype(BF16)
+                    fine_edge(j).start()
+
+                @pl.when(is2)
+                def _():
+                    fine_edge(j).wait_recv()
+                    fsb[j] = (both + fra[j].astype(F32)).astype(BF16)
+                    fine_inner(j).start()
+
+                @pl.when(is1)
+                def _():
+                    fine_edge(j).wait_recv()
+                    fine_inner(j).wait_recv()
+                    ftot[j] = (both + fra[j].astype(F32) + frb[j].astype(F32)).astype(BF16)
+                    fine_send(j)
+
+                return 0
+
+            lax.fori_loop(0, PIECES, body, 0)
+
+    def fine_arrive(k):
+        @pl.when((k >= coarse) & (k < units) & (z != 1))
+        def _():
+            def body(i, _):
+                j = (k - coarse) * PIECES + i
+                fine_down(j).wait_recv()
+                fine_send(j)
+                return 0
+
+            lax.fori_loop(0, PIECES, body, 0)
+
+    def fine_end():
+        def body(j, _):
+            keep, give = fine_out(j)
+            keep.wait()
+            give.wait_send()
+
+            @pl.when(is0 | is3)
+            def _():
+                fine_edge(j).wait_send()
+
+            @pl.when(is2)
+            def _():
+                fine_inner(j).wait_send()
+
+            @pl.when(is1)
+            def _():
+                fine_down(j).wait_send()
+
+            @pl.when(is1 | is2)
+            def _():
+                fine_up(j).wait_send()
+
+            return 0
+
+        lax.fori_loop(0, FINE * PIECES, body, 0)
+
     def load(k):
-        @pl.when(inside(k))
+        @pl.when((k >= 0) & (k < units))
         def _():
             @pl.when(k % UNITS == 0)
             def _():
@@ -432,6 +542,8 @@
         add(now - sum_lag)
         arrive(now - tot_lag)
         send(now - sum_lag, now - tot_lag)
+        fine_add(now - sum_lag)
+        fine_arrive(now - tot_lag)
         load(now - sum_lag + 1)
 
         @pl.when(i < STEPS)
@@ -459,7 +571,7 @@
 
     lax.fori_loop(0, max(FIRST + units + 12, STEPS + 2), tick, 0)
 
-    for k in range(units - SEND_SLOTS, units):
+    for k in range(coarse - SEND_SLOTS, coarse):
 
         @pl.when(is0 | is3)
         def _(k=k):
@@ -469,6 +581,7 @@
         def _(k=k):
             s_copy_inner(k).wait_send()
 
+    fine_end()
     pltpu.make_async_copy(theirs_hbm, theirs_hbm, partner_sem).wait()
 
 
@@ -507,6 +620,7 @@
             pltpu.VMEM((SLOTS, r, d), BF16),
             pltpu.VMEM((SLOTS, r, d), BF16),
             pltpu.VMEM((SLOTS, r, d), BF16),
+            *[pltpu.VMEM((FINE * PIECES, r // PIECES, d), BF16)] * 4,
             dma((4,)),
             dma((2, 3)),
             dma((2,)),
@@ -523,6 +637,7 @@
             dma((SLOTS,)),
             dma((SLOTS,)),
             dma,
+            *[dma((FINE * PIECES,))] * 8,
         ],
         compiler_params=pltpu.CompilerParams(collective_id=0, has_side_effects=True, vmem_limit_bytes=VMEM_LIMIT),
         cost_estimate=pl.CostEstimate(flops=2 * 15 * t * d * ff, bytes_accessed=100 * d * ff, transcendentals=2 * t * ff),

time: 624 us -> 624 us (level)
  no operation moved by 1% of the time
where the time goes in v5:
time: 624 us
  Pallas kernels  609 us (98%)
  between operations  14.1 us (2%)
    pallas_call x1, Pallas kernels, backward(): pl.pallas_call(backward_kernel, out_shape=[jax.ShapeDtypeStruct((SUMMED,...  416 us
    pallas_call x2, Pallas kernels, adamw(): pl.pallas_call(functools.partial(adamw_kernel, tuple(rounds), first, len(...  141 us
    pallas_call x1, Pallas kernels, forward(): pl.pallas_call(functools.partial(forward_kernel, width), grid=(t // tile,...  51.6 us
  transfers between devices with their start and end apart: 1, of which 0 were waited for; matrix products, arithmetic and copies ran while one was open for 0% of the time, Pallas kernels for 19%

profile of v5, /device:TPU:27, one launch (start us, length us, event | category | flops | bytes accessed | tf_op | source)
XLA Modules:
  0.0 623.6 jit_solution(11077070153444584931)
XLA Ops:
  7.2 0.0 all-reduce.2.cloned.1.call-start
  7.2 51.6 %forward.1 = (bf16[2048,1024]{1,0:T(8,128)(2,1)}, bf16[2048,1024]{1,0:T(8,128)(2,1)}, bf16[2048,1024]{1,0:T(8,128)(2,1)}) custom-call(bf16[2048,1024]{1,0:T(8,128)(2,1)} %bitcast.2, bf16[2,1024,3200]{2,1,0:T(8,128)(2,1)} %refs_0_.3, bf16[2,1024,3200]{2,1,0:T(8,128)(2,1)} %refs_3_.3, bf16[2,3200,1024]{2,1,0:T(8,128)(2,1)} %refs_6_.3), custom_call_target="tpu_custom_call" | custom-call | flops 40265318400 | bytes 36438016 | tf_op jit(solution)/shard_map/forward/pallas_call | solution.py:89
  58.9 416.4 %backward.1 = (bf16[26,640,1024]{2,1,0:T(8,128)(2,1)}, bf16[4,640,1024]{2,1,0:T(8,128)(2,1)}, bf16[52,160,1024]{2,1,0:T(8,128)(2,1)}, bf16[52,160,1024]{2,1,0:T(8,128)(2,1)}) custom-call(bf16[2048,1024]{1,0:T(8,128)(2,1)} %get-tuple-element.32.a1_hbm, bf16[2048,1024]{1,0:T(8,128)(2,1)} %get-tuple-element.33.a0_hbm, ...), custom_call_target="tpu_custom_call" | custom-call | flops 201326592000 | bytes 327680000 | tf_op jit(solution)/shard_map/backward/pallas_call | solution.py:597
  475.3 0.0 all-reduce.2.cloned.1.call-update
  475.3 121.5 %adamw.2 = (bf16[2,1024,3200]{2,1,0:T(8,128)(2,1)}, f32[2,1024,3200]{2,1,0:T(8,128)}, f32[2,1024,3200]{2,1,0:T(8,128)}, bf16[2,1024,3200]{2,1,0:T(8,128)(2,1)}, ...) custom-call(bf16[2,1024,3200]{2,1,0:T(8,128)(2,1)} %refs_0_.3, ...), custom_call_target="tpu_custom_call" | custom-call | flops 34078720000 | bytes 374865920 | tf_op jit(solution)/shard_map/adamw/pallas_call | solution.py:782
  596.9 0.0 all-reduce.2.cloned.1.call-done.refs_9_
  596.9 19.9 %adamw.3 = (bf16[2,1024,3200]{2,1,0:T(8,128)(2,1)}, f32[2,1024,3200]{2,1,0:T(8,128)}, f32[2,1024,3200]{2,1,0:T(8,128)}, bf16[2,1024,3200]{2,1,0:T(8,128)(2,1)}, ...) custom-call(bf16[2,1024,3200]{2,1,0:T(8,128)(2,1)} %refs_0_.3, ...), custom_call_target="tpu_custom_call", output_to_operand_aliasing={{0}: (10, {}), {1}: (11, {}), {2}: (12, {}), {3}: (13, {}),... | custom-call | flops 5242880000 | bytes 57671680 | tf_op jit(solution)/shard_map/adamw/pallas_call | solution.py:782
Async XLA Ops:
  7.2 589.7 %all-reduce.2.cloned.1.call-start = ((), (), s32[]{:S(2)}) async-start(), calls=%async_computation | async-start | bytes 10485760 | tf_op jit(solution)/shard_map/psum | solution.py:819
Sparse Core Ops, SparseCore 0:
  475.5 115.5 all-reduce.1

commit v6 on v5

--- a/solution.py
+++ b/solution.py
@@ -15,7 +15,7 @@
 SUMMED = 26
 UNITS = 2
 FINE, PIECES = 2, 5
-FIRST = 4
+FIRST = 5
 SLOTS, SEND_SLOTS, LOAD_SLOTS = 12, 6, 4
 NN = (((1,), (0,)), ((), ()))
 NT = (((1,), (1,)), ((), ()))
@@ -108,14 +108,23 @@
 HALF_STEPS, DA_STEPS, TILES = 4, 2, 4
 BLOCK_STEPS, LOW_STEPS = 2 * HALF_STEPS + DA_STEPS, 2 * HALF_STEPS
 TURN = BLOCKS * BLOCK_STEPS
-STEPS = TURN + DA_STEPS + BLOCKS * LOW_STEPS
+STEPS = 1 + TURN + DA_STEPS + BLOCKS * LOW_STEPS
 
 
 def step_of(s):
-    low = s - (TURN + DA_STEPS)
-    block = jnp.where(s < TURN, s // BLOCK_STEPS, jnp.where(low < 0, BLOCKS, BLOCKS + low // LOW_STEPS))
-    place = jnp.where(s < TURN, s % BLOCK_STEPS, jnp.where(low < 0, BLOCK_STEPS + s - TURN, low % LOW_STEPS))
-    return block, place
+    p = jnp.where(s <= 3, s, s - 1)
+    low = p - (TURN + DA_STEPS)
+    block = jnp.where(p < TURN, p // BLOCK_STEPS, jnp.where(low < 0, BLOCKS, BLOCKS + low // LOW_STEPS))
+    place = jnp.where(p < TURN, p % BLOCK_STEPS, jnp.where(low < 0, BLOCK_STEPS + p - TURN, low % LOW_STEPS))
+    half = jnp.where(place < LOW_STEPS, place // HALF_STEPS, 0)
+    kind = jnp.where(place < LOW_STEPS, place % HALF_STEPS, place - 2)
+    return block, half, jnp.where(s == 3, 4, jnp.where(s == 4, 5, kind))
+
+
+def made_in(kind):
+    low = jnp.where((kind == 3) | (kind == 4), 1, jnp.where(kind == 5, 2, 0))
+    high = jnp.where((kind == 3) | (kind == 5), 3, jnp.where(kind == 4, 2, jnp.where(kind == 2, 1, 0)))
+    return low, high
 
 
 def summed_piece(c):
@@ -187,10 +196,10 @@
     def at_half(half):
         return pl.ds(pl.multiple_of(half * fs, fs), fs)
 
-    def hidden(block, half):
+    def hidden(block, half, tokens):
         slot = block % 2
 
-        @pl.when(half == 0)
+        @pl.when((half == 0) & (tokens == 0))
         def _():
             @pl.when(block == 0)
             def _():
@@ -213,8 +222,8 @@
             wut[...] = wub[slot].T
 
         units_at = at_half(half)
-        for i in range(TILES):
-            at = pl.ds(i * sub, sub)
+        for i in range(TILES // 2):
+            at = pl.ds(pl.multiple_of((tokens * (TILES // 2) + i) * sub, sub), sub)
             gate = dot(wgt[units_at, :], ad[1, at, :], NT)
             up = dot(wut[units_at, :], ad[1, at, :], NT)
             dp = dot(wdb[slot, units_at, :], ad[0, at, :], NT).astype(BF16).astype(F32)
@@ -224,9 +233,12 @@
             pgu[1, units_at, at] = (dp * up * (sig + silu * (1.0 - sig))).astype(BF16)
             pgu[2, units_at, at] = (dp * silu).astype(BF16)
 
-    def gradient(block, half, which):
-        rhs = jnp.minimum(which, 1)
-        stage[slot_of(half, which)] = dot(pgu[which, at_half(half), :], ad[rhs]).astype(BF16)
+    def gradients(half, kind):
+        def body(which, _):
+            stage[which] = dot(pgu[which, at_half(half), :], ad[jnp.minimum(which, 1)]).astype(BF16)
+            return 0
+
+        lax.fori_loop(*made_in(kind), body, 0)
 
     def to_input(block, step):
         slot = block % 2
@@ -262,9 +274,6 @@
         def _():
             load_a0.start()
 
-    def slot_of(half, which):
-        return (half + which) % 2
-
     def rows(slot, c):
         return stage.at[slot, pl.ds(pl.multiple_of(c * part, part), part), :]
 
@@ -278,7 +287,7 @@
         return pltpu.make_async_copy(stage.at[slot], left_hbm.at[3 * block + which - SUMMED, at_half(half), :], left_sem.at[slot])
 
     def stage_copies(block, half, which, go):
-        slot, here = slot_of(half, which), 3 * block + which < SUMMED
+        slot, here = which, 3 * block + which < SUMMED
 
         @pl.when(here)
         def _():
@@ -300,7 +309,7 @@
 
     is0, is1, is2, is3 = z == 0, z == 1, z == 2, z == 3
     sum_lag = jnp.where(is1, 2, jnp.where(is2, 1, 0))
-    tot_lag = jnp.where(is1, 2, jnp.where(is3, 9, 6))
+    tot_lag = jnp.where(is1, 2, jnp.where(is3, 9, jnp.where(is2, 5, 6)))
     free_lag = tot_lag + jnp.where(is3, 2, 3)
 
     def load_copies(k):
@@ -527,12 +536,13 @@
     def stage_of(s, go):
         @pl.when((s >= 0) & (s < STEPS))
         def _():
-            block, place = step_of(s)
-            half, kind = place // HALF_STEPS, place % HALF_STEPS
-
-            @pl.when((place < LOW_STEPS) & (kind >= 1))
-            def _():
-                stage_copies(block, half, kind - 1, go)
+            block, half, kind = step_of(s)
+
+            def body(which, _):
+                stage_copies(block, half, which, go)
+                return 0
+
+            lax.fori_loop(*made_in(kind), body, 0)
 
     def tick(i, _):
         stage_of(i - 2, False)
@@ -548,24 +558,23 @@
 
         @pl.when(i < STEPS)
         def _():
-            block, place = step_of(i)
-            half, kind = place // HALF_STEPS, place % HALF_STEPS
-
-            @pl.when((place < LOW_STEPS) & (kind == 0))
-            def _():
-                hidden(block, half)
-
-            @pl.when((place < LOW_STEPS) & (kind >= 1))
-            def _():
-                gradient(block, half, kind - 1)
-
-            @pl.when((place >= LOW_STEPS) & (place < BLOCK_STEPS))
-            def _():
-                to_input(block, place - LOW_STEPS)
-
-            @pl.when(place >= BLOCK_STEPS)
-            def _():
-                turn(place - BLOCK_STEPS)
+            block, half, kind = step_of(i)
+
+            @pl.when(kind < 2)
+            def _():
+                hidden(block, half, kind)
+
+            @pl.when((kind >= 2) & (kind <= 5))
+            def _():
+                gradients(half, kind)
+
+            @pl.when((kind == 6) | (kind == 7))
+            def _():
+                to_input(block, kind - 6)
+
+            @pl.when(kind >= 8)
+            def _():
+                turn(kind - 8)
 
         return 0
 
@@ -613,7 +622,7 @@
             pltpu.VMEM((f, d), BF16),
             pltpu.VMEM((f, d), BF16),
             pltpu.VMEM((TILES, d, sub), F32),
-            pltpu.VMEM((2, fs, d), BF16),
+            pltpu.VMEM((3, fs, d), BF16),
             pltpu.VMEM((LOAD_SLOTS, r, d), BF16),
             pltpu.VMEM((LOAD_SLOTS, r, d), BF16),
             pltpu.VMEM((SEND_SLOTS, r, d), BF16),
@@ -623,10 +632,10 @@
             *[pltpu.VMEM((FINE * PIECES, r // PIECES, d), BF16)] * 4,
             dma((4,)),
             dma((2, 3)),
-            dma((2,)),
-            dma((2,)),
+            dma((3,)),
+            dma((3,)),
             dma((2 * SUMMED,)),
-            dma((2,)),
+            dma((3,)),
             dma((LOAD_SLOTS, 2)),
             dma((SEND_SLOTS,)),
             dma((SLOTS,)),

time: 624 us -> 615 us (0.986)
  Pallas kernels: 609 us -> 600 us
    pallas_call x1, Pallas kernels: 416 us -> 407 us  [backward(): pl.pallas_call(backward_kernel, out_shape=[jax.ShapeDtypeStruct((SUMMED,...]
  transfers between devices with their start and end apart: 1 -> 1, of which waited for: 0 -> 0; matrix products, arithmetic and copies ran while one was open for 0% -> 0% of each run, Pallas kernels for 19% -> 20%
where the time goes in v6:
time: 615 us; the launch traced here: 614 us
  Pallas kernels  600 us (98%)
  between operations  14.1 us (2%)
    pallas_call x1, Pallas kernels, backward(): pl.pallas_call(backward_kernel, out_shape=[jax.ShapeDtypeStruct((SUMMED,...  407 us
    pallas_call x2, Pallas kernels, adamw(): pl.pallas_call(functools.partial(adamw_kernel, tuple(rounds), first, len(...  141 us
    pallas_call x1, Pallas kernels, forward(): pl.pallas_call(functools.partial(forward_kernel, width), grid=(t // tile,...  51.6 us
  transfers between devices with their start and end apart: 1, of which 0 were waited for; matrix products, arithmetic and copies ran while one was open for 0% of the time, Pallas kernels for 20%

profile of v6, /device:TPU:27, one launch (start us, length us, event | category | flops | bytes accessed | tf_op | source)
XLA Modules:
  0.0 614.4 jit_solution(17185561598944839049)
XLA Ops:
  7.2 0.0 all-reduce.2.cloned.1.call-start
  7.2 51.6 %forward.1 = (bf16[2048,1024]{1,0:T(8,128)(2,1)}, bf16[2048,1024]{1,0:T(8,128)(2,1)}, bf16[2048,1024]{1,0:T(8,128)(2,1)}) custom-call(bf16[2048,1024]{1,0:T(8,128)(2,1)} %bitcast.2, bf16[2,1024,3200]{2,1,0:T(8,128)(2,1)} %refs_0_.3, bf16[2,1024,3200]{2,1,0:T(8,128)(2,1)} %refs_3_.3, bf16[2,3200,1024]{2,1,0:T(8,128)(2,1)} %refs_6_.3), custom_call_target="tpu_custom_call" | custom-call | flops 40265318400 | bytes 36438016 | tf_op jit(solution)/shard_map/forward/pallas_call | solution.py:89
  58.9 407.2 %backward.1 = (bf16[26,640,1024]{2,1,0:T(8,128)(2,1)}, bf16[4,640,1024]{2,1,0:T(8,128)(2,1)}, bf16[52,160,1024]{2,1,0:T(8,128)(2,1)}, bf16[52,160,1024]{2,1,0:T(8,128)(2,1)}) custom-call(bf16[2048,1024]{1,0:T(8,128)(2,1)} %get-tuple-element.32.a1_hbm, bf16[2048,1024]{1,0:T(8,128)(2,1)} %get-tuple-element.33.a0_hbm, ...), custom_call_target="tpu_custom_call" | custom-call | flops 201326592000 | bytes 327680000 | tf_op jit(solution)/shard_map/backward/pallas_call | solution.py:606
  466.1 0.0 all-reduce.2.cloned.1.call-update
  466.1 121.5 %adamw.2 = (bf16[2,1024,3200]{2,1,0:T(8,128)(2,1)}, f32[2,1024,3200]{2,1,0:T(8,128)}, f32[2,1024,3200]{2,1,0:T(8,128)}, bf16[2,1024,3200]{2,1,0:T(8,128)(2,1)}, ...) custom-call(bf16[2,1024,3200]{2,1,0:T(8,128)(2,1)} %refs_0_.3, ...), custom_call_target="tpu_custom_call" | custom-call | flops 34078720000 | bytes 374865920 | tf_op jit(solution)/shard_map/adamw/pallas_call | solution.py:791
  587.6 0.0 all-reduce.2.cloned.1.call-done.refs_9_
  587.6 19.9 %adamw.3 = (bf16[2,1024,3200]{2,1,0:T(8,128)(2,1)}, f32[2,1024,3200]{2,1,0:T(8,128)}, f32[2,1024,3200]{2,1,0:T(8,128)}, bf16[2,1024,3200]{2,1,0:T(8,128)(2,1)}, ...) custom-call(bf16[2,1024,3200]{2,1,0:T(8,128)(2,1)} %refs_0_.3, ...), custom_call_target="tpu_custom_call", output_to_operand_aliasing={{0}: (10, {}), {1}: (11, {}), {2}: (12, {}), {3}: (13, {}),... | custom-call | flops 5242880000 | bytes 57671680 | tf_op jit(solution)/shard_map/adamw/pallas_call | solution.py:791
Async XLA Ops:
  7.2 580.4 %all-reduce.2.cloned.1.call-start = ((), (), s32[]{:S(2)}) async-start(), calls=%async_computation | async-start | bytes 10485760 | tf_op jit(solution)/shard_map/psum | solution.py:828
Sparse Core Ops, SparseCore 0:
  466.2 115.5 all-reduce.1

commit v7 on v6

--- a/solution.py
+++ b/solution.py
@@ -6,6 +6,7 @@
 from jax.experimental import pallas as pl
 from jax.experimental.pallas import tpu as pltpu
 from jax.sharding import PartitionSpec as P
+
 
 BF16, F32 = jnp.bfloat16, jnp.float32
 MESH = pl.DeviceIdType.MESH
@@ -29,51 +30,53 @@
     return lax.rsqrt(jnp.mean(wide * wide, -1, keepdims=True) + 1e-6)
 
 
-def cuts(n, width):
-    starts = list(range(0, n - width + 1, width))
-    return [(s, (starts[i + 1] if i + 1 < len(starts) else n) - s) for i, s in enumerate(starts)]
-
-
-def forward_kernel(width, x_ref, wg_hbm, wu_hbm, wd_hbm, a0_ref, h1_ref, a1_ref, wg, wu, wd, p, sems):
+def groups_of(ff):
+    width = min(ff, 512)
+    starts = list(range(0, ff - width + 1, width))
+    pieces = [(s, (starts[i + 1] if i + 1 < len(starts) else ff) - s) for i, s in enumerate(starts)]
+    return [g for g in (pieces[:1], pieces[1:3], pieces[3:]) if g]
+
+
+def forward_kernel(groups, x_ref, wg_hbm, wu_hbm, wd_hbm, a0_ref, h1_ref, a1_ref, wg, wu, wd, p, sems):
     first = pl.program_id(0) == 0
-    pieces = cuts(wg.shape[1], width)
 
     def loads(i):
-        s, n = pieces[i]
+        at = pl.ds(groups[i][0][0], sum(n for _, n in groups[i]))
         return (
-            pltpu.make_async_copy(wg_hbm.at[0, :, pl.ds(s, n)], wg.at[:, pl.ds(s, n)], sems.at[0, i]),
-            pltpu.make_async_copy(wu_hbm.at[0, :, pl.ds(s, n)], wu.at[:, pl.ds(s, n)], sems.at[1, i]),
-            pltpu.make_async_copy(wd_hbm.at[0, pl.ds(s, n), :], wd.at[pl.ds(s, n), :], sems.at[2, i]),
+            pltpu.make_async_copy(wg_hbm.at[0, :, at], wg.at[:, at], sems.at[0, i]),
+            pltpu.make_async_copy(wu_hbm.at[0, :, at], wu.at[:, at], sems.at[1, i]),
+            pltpu.make_async_copy(wd_hbm.at[0, at, :], wd.at[at, :], sems.at[2, i]),
         )
+
+    everything = range(len(groups))
 
     @pl.when(first)
     def _():
-        for i in range(len(pieces)):
+        for i in everything:
             for c in loads(i)[:2]:
                 c.start()
-        for i in range(len(pieces)):
+        for i in everything:
             loads(i)[2].start()
 
     wide = x_ref[...].astype(F32)
     a = (wide * scale_of(wide)).astype(BF16)
     a0_ref[...] = a
-    for i, (s, n) in enumerate(pieces):
+    for i in everything:
 
         @pl.when(first)
         def _(i=i):
             for c in loads(i)[:2]:
                 c.wait()
-
-        gate = dot(a, wg[:, s : s + n])
-        up = dot(a, wu[:, s : s + n])
-        p[:, s : s + n] = (gate * (0.5 * jnp.tanh(0.5 * gate) + 0.5) * up).astype(BF16)
-
-    @pl.when(first)
-    def _():
-        for i in range(len(pieces)):
-            loads(i)[2].wait()
-
-    h1 = (wide + dot(p[...], wd[...]).astype(BF16).astype(F32)).astype(BF16)
+            if i + 1 == len(groups):
+                for j in everything:
+                    loads(j)[2].wait()
+
+        for s, n in groups[i]:
+            gate = dot(a, wg[:, s : s + n])
+            up = dot(a, wu[:, s : s + n])
+            p[:, s : s + n] = (gate * (0.5 * jnp.tanh(0.5 * gate) + 0.5) * up).astype(BF16)
+
+    h1 = (x_ref[...].astype(F32) + dot(p[...], wd[...]).astype(BF16).astype(F32)).astype(BF16)
     h1_ref[...] = h1
     wide1 = h1.astype(F32)
     a1_ref[...] = (wide1 * scale_of(wide1)).astype(BF16)
@@ -83,11 +86,11 @@
     t, d = x.shape
     ff = wg.shape[2]
     tile = min(t, 1024)
-    width = min(ff, 768)
+    groups = groups_of(ff)
     rows = pl.BlockSpec((tile, d), lambda i: (i, 0))
     anywhere = pl.BlockSpec(memory_space=pl.ANY)
     return pl.pallas_call(
-        functools.partial(forward_kernel, width),
+        functools.partial(forward_kernel, groups),
         grid=(t // tile,),
         out_shape=[jax.ShapeDtypeStruct((t, d), BF16)] * 3,
         in_specs=[rows, anywhere, anywhere, anywhere],
@@ -97,7 +100,7 @@
             pltpu.VMEM((d, ff), BF16),
             pltpu.VMEM((ff, d), BF16),
             pltpu.VMEM((tile, ff), BF16),
-            pltpu.SemaphoreType.DMA((3, len(cuts(ff, width)))),
+            pltpu.SemaphoreType.DMA((3, len(groups))),
         ],
         compiler_params=pltpu.CompilerParams(vmem_limit_bytes=VMEM_LIMIT, dimension_semantics=("arbitrary",)),
         cost_estimate=pl.CostEstimate(flops=6 * t * d * ff, bytes_accessed=6 * d * ff + 8 * t * d, transcendentals=t * ff),
@@ -169,15 +172,22 @@
             pltpu.make_async_copy(wd_hbm.at[layer, at, :], wdb.at[slot], w_sem.at[slot, 2]),
         )
 
-    load_dy = pltpu.make_async_copy(dy_hbm, ad.at[0], in_sem.at[0])
-    load_a1 = pltpu.make_async_copy(a1_hbm, ad.at[1], in_sem.at[1])
-    load_h1 = pltpu.make_async_copy(h1_hbm, ad.at[1], in_sem.at[2])
-    load_a0 = pltpu.make_async_copy(a0_hbm, ad.at[1], in_sem.at[3])
-
-    load_a1.start()
-    for c in weights(0):
+    def load_tokens(which):
+        at = pl.ds(which * (t // 2), t // 2)
+        return (
+            pltpu.make_async_copy(a1_hbm.at[at, :], ad.at[1, at, :], in_sem.at[0, which]),
+            pltpu.make_async_copy(dy_hbm.at[at, :], ad.at[0, at, :], in_sem.at[1, which]),
+        )
+
+    load_h1 = pltpu.make_async_copy(h1_hbm, ad.at[1], in_sem.at[2, 0])
+    load_a0 = pltpu.make_async_copy(a0_hbm, ad.at[1], in_sem.at[3, 0])
+
+    for a, b in zip(weights(0), (*load_tokens(0), None)):
+        a.start()
+        if b is not None:
+            b.start()
+    for c in load_tokens(1):
         c.start()
-    load_dy.start()
     dat[...] = jnp.zeros_like(dat)
 
     barrier = pltpu.get_barrier_semaphore()
@@ -199,13 +209,15 @@
     def hidden(block, half, tokens):
         slot = block % 2
 
+        for which in range(2):
+
+            @pl.when((block == 0) & (half == 0) & (tokens == which))
+            def _(which=which):
+                for c in load_tokens(which):
+                    c.wait()
+
         @pl.when((half == 0) & (tokens == 0))
         def _():
-            @pl.when(block == 0)
-            def _():
-                load_a1.wait()
-                load_dy.wait()
-
             @pl.when(block == BLOCKS)
             def _():
                 load_a0.wait()
@@ -630,7 +642,7 @@
             pltpu.VMEM((SLOTS, r, d), BF16),
             pltpu.VMEM((SLOTS, r, d), BF16),
             *[pltpu.VMEM((FINE * PIECES, r // PIECES, d), BF16)] * 4,
-            dma((4,)),
+            dma((4, 2)),
             dma((2, 3)),
             dma((3,)),
             dma((3,)),

time: 615 us -> 615 us (level)
  no operation moved by 1% of the time
where the time goes in v7:
time: 615 us; the launch traced here: 614 us
  Pallas kernels  600 us (98%)
  between operations  14.1 us (2%)
    pallas_call x1, Pallas kernels, backward(): pl.pallas_call(backward_kernel, out_shape=[jax.ShapeDtypeStruct((SUMMED,...  407 us
    pallas_call x2, Pallas kernels, adamw(): pl.pallas_call(functools.partial(adamw_kernel, tuple(rounds), first, len(...  143 us
    pallas_call x1, Pallas kernels, forward(): pl.pallas_call(functools.partial(forward_kernel, groups), grid=(t // tile...  50.8 us
  transfers between devices with their start and end apart: 1, of which 0 were waited for; matrix products, arithmetic and copies ran while one was open for 0% of the time, Pallas kernels for 20%

profile of v7, /device:TPU:27, one launch (start us, length us, event | category | flops | bytes accessed | tf_op | source)
XLA Modules:
  0.0 614.4 jit_solution(14058758480927350593)
XLA Ops:
  7.2 0.0 all-reduce.2.cloned.1.call-start
  7.2 50.8 %forward.1 = (bf16[2048,1024]{1,0:T(8,128)(2,1)}, bf16[2048,1024]{1,0:T(8,128)(2,1)}, bf16[2048,1024]{1,0:T(8,128)(2,1)}) custom-call(bf16[2048,1024]{1,0:T(8,128)(2,1)} %bitcast.2, bf16[2,1024,3200]{2,1,0:T(8,128)(2,1)} %refs_0_.3, bf16[2,1024,3200]{2,1,0:T(8,128)(2,1)} %refs_3_.3, bf16[2,3200,1024]{2,1,0:T(8,128)(2,1)} %refs_6_.3), custom_call_target="tpu_custom_call" | custom-call | flops 40265318400 | bytes 36438016 | tf_op jit(solution)/shard_map/forward/pallas_call | solution.py:92
  58.0 406.7 %backward.1 = (bf16[26,640,1024]{2,1,0:T(8,128)(2,1)}, bf16[4,640,1024]{2,1,0:T(8,128)(2,1)}, bf16[52,160,1024]{2,1,0:T(8,128)(2,1)}, bf16[52,160,1024]{2,1,0:T(8,128)(2,1)}) custom-call(bf16[2048,1024]{1,0:T(8,128)(2,1)} %get-tuple-element.32.a1_hbm, bf16[2048,1024]{1,0:T(8,128)(2,1)} %get-tuple-element.33.a0_hbm, ...), custom_call_target="tpu_custom_call" | custom-call | flops 201326592000 | bytes 327680000 | tf_op jit(solution)/shard_map/backward/pallas_call | solution.py:618
  464.7 0.0 all-reduce.2.cloned.1.call-update
  464.8 122.8 %adamw.2 = (bf16[2,1024,3200]{2,1,0:T(8,128)(2,1)}, f32[2,1024,3200]{2,1,0:T(8,128)}, f32[2,1024,3200]{2,1,0:T(8,128)}, bf16[2,1024,3200]{2,1,0:T(8,128)(2,1)}, ...) custom-call(bf16[2,1024,3200]{2,1,0:T(8,128)(2,1)} %refs_0_.3, ...), custom_call_target="tpu_custom_call" | custom-call | flops 34078720000 | bytes 374865920 | tf_op jit(solution)/shard_map/adamw/pallas_call | solution.py:803
  587.6 0.0 all-reduce.2.cloned.1.call-done.refs_9_
  587.6 19.9 %adamw.3 = (bf16[2,1024,3200]{2,1,0:T(8,128)(2,1)}, f32[2,1024,3200]{2,1,0:T(8,128)}, f32[2,1024,3200]{2,1,0:T(8,128)}, bf16[2,1024,3200]{2,1,0:T(8,128)(2,1)}, ...) custom-call(bf16[2,1024,3200]{2,1,0:T(8,128)(2,1)} %refs_0_.3, ...), custom_call_target="tpu_custom_call", output_to_operand_aliasing={{0}: (10, {}), {1}: (11, {}), {2}: (12, {}), {3}: (13, {}),... | custom-call | flops 5242880000 | bytes 57671680 | tf_op jit(solution)/shard_map/adamw/pallas_call | solution.py:803
Async XLA Ops:
  7.2 580.5 %all-reduce.2.cloned.1.call-start = ((), (), s32[]{:S(2)}) async-start(), calls=%async_computation | async-start | bytes 10485760 | tf_op jit(solution)/shard_map/psum | solution.py:840
Sparse Core Ops, SparseCore 0:
  464.9 115.7 all-reduce.1

commit v8 on v7

--- a/solution.py
+++ b/solution.py
@@ -6,7 +6,6 @@
 from jax.experimental import pallas as pl
 from jax.experimental.pallas import tpu as pltpu
 from jax.sharding import PartitionSpec as P
-
 
 BF16, F32 = jnp.bfloat16, jnp.float32
 MESH = pl.DeviceIdType.MESH
@@ -31,52 +30,70 @@
 
 
 def groups_of(ff):
-    width = min(ff, 512)
-    starts = list(range(0, ff - width + 1, width))
-    pieces = [(s, (starts[i + 1] if i + 1 < len(starts) else ff) - s) for i, s in enumerate(starts)]
-    return [g for g in (pieces[:1], pieces[1:3], pieces[3:]) if g]
-
-
-def forward_kernel(groups, x_ref, wg_hbm, wu_hbm, wd_hbm, a0_ref, h1_ref, a1_ref, wg, wu, wd, p, sems):
-    first = pl.program_id(0) == 0
+    shared = ff - 128 if ff % 512 == 128 and ff > 512 else None
+    end = ff if shared is None else shared
+    width = min(end, 512)
+    starts = list(range(0, end - width + 1, width))
+    pieces = [(s, (starts[i + 1] if i + 1 < len(starts) else end) - s) for i, s in enumerate(starts)]
+    return [g for g in (pieces[:2], pieces[2:]) if g], shared
+
+
+def forward_kernel(groups, shared, x_hbm, wg_hbm, wu_hbm, wd_hbm, a0_ref, h1_ref, a1_ref, x, wg, wu, both, wd, p, sems, x_sem):
+    tile, tiles = a0_ref.shape[0], x.shape[0]
+    now = pl.program_id(0)
+    first = now == 0
+
+    def load_x(i):
+        return pltpu.make_async_copy(x_hbm.at[pl.ds(i * tile, tile), :], x.at[i], x_sem.at[i])
 
     def loads(i):
         at = pl.ds(groups[i][0][0], sum(n for _, n in groups[i]))
-        return (
+        copies = [
             pltpu.make_async_copy(wg_hbm.at[0, :, at], wg.at[:, at], sems.at[0, i]),
             pltpu.make_async_copy(wu_hbm.at[0, :, at], wu.at[:, at], sems.at[1, i]),
-            pltpu.make_async_copy(wd_hbm.at[0, at, :], wd.at[at, :], sems.at[2, i]),
-        )
-
-    everything = range(len(groups))
+        ]
+        if shared is not None and i + 1 == len(groups):
+            for k, w_hbm in enumerate((wg_hbm, wu_hbm)):
+                half = both.at[:, pl.ds(k * 128, 128)]
+                copies.append(pltpu.make_async_copy(w_hbm.at[0, :, pl.ds(shared, 128)], half, sems.at[2, k]))
+        return copies
+
+    load_down = pltpu.make_async_copy(wd_hbm.at[0], wd, sems.at[3, 0])
 
     @pl.when(first)
     def _():
-        for i in everything:
-            for c in loads(i)[:2]:
+        load_x(0).start()
+        for i in range(len(groups)):
+            for c in loads(i):
                 c.start()
-        for i in everything:
-            loads(i)[2].start()
-
-    wide = x_ref[...].astype(F32)
+        load_down.start()
+        for i in range(1, tiles):
+            load_x(i).start()
+
+    load_x(now).wait()
+    wide = x[now].astype(F32)
     a = (wide * scale_of(wide)).astype(BF16)
     a0_ref[...] = a
-    for i in everything:
+
+    def product(gate, up):
+        return (gate * (0.5 * jnp.tanh(0.5 * gate) + 0.5) * up).astype(BF16)
+
+    for i in range(len(groups)):
 
         @pl.when(first)
         def _(i=i):
-            for c in loads(i)[:2]:
+            for c in loads(i):
                 c.wait()
             if i + 1 == len(groups):
-                for j in everything:
-                    loads(j)[2].wait()
+                load_down.wait()
 
         for s, n in groups[i]:
-            gate = dot(a, wg[:, s : s + n])
-            up = dot(a, wu[:, s : s + n])
-            p[:, s : s + n] = (gate * (0.5 * jnp.tanh(0.5 * gate) + 0.5) * up).astype(BF16)
-
-    h1 = (x_ref[...].astype(F32) + dot(p[...], wd[...]).astype(BF16).astype(F32)).astype(BF16)
+            p[:, s : s + n] = product(dot(a, wg[:, s : s + n]), dot(a, wu[:, s : s + n]))
+    if shared is not None:
+        gate_up = dot(a, both[...])
+        p[:, shared:] = product(gate_up[:, :128], gate_up[:, 128:])
+
+    h1 = (x[now].astype(F32) + dot(p[...], wd[...]).astype(BF16).astype(F32)).astype(BF16)
     h1_ref[...] = h1
     wide1 = h1.astype(F32)
     a1_ref[...] = (wide1 * scale_of(wide1)).astype(BF16)
@@ -86,21 +103,23 @@
     t, d = x.shape
     ff = wg.shape[2]
     tile = min(t, 1024)
-    groups = groups_of(ff)
-    rows = pl.BlockSpec((tile, d), lambda i: (i, 0))
+    groups, shared = groups_of(ff)
     anywhere = pl.BlockSpec(memory_space=pl.ANY)
     return pl.pallas_call(
-        functools.partial(forward_kernel, groups),
+        functools.partial(forward_kernel, groups, shared),
         grid=(t // tile,),
         out_shape=[jax.ShapeDtypeStruct((t, d), BF16)] * 3,
-        in_specs=[rows, anywhere, anywhere, anywhere],
-        out_specs=[rows] * 3,
+        in_specs=[anywhere] * 4,
+        out_specs=[pl.BlockSpec((tile, d), lambda i: (i, 0))] * 3,
         scratch_shapes=[
+            pltpu.VMEM((t // tile, tile, d), BF16),
             pltpu.VMEM((d, ff), BF16),
             pltpu.VMEM((d, ff), BF16),
+            pltpu.VMEM((d, 256), BF16),
             pltpu.VMEM((ff, d), BF16),
             pltpu.VMEM((tile, ff), BF16),
-            pltpu.SemaphoreType.DMA((3, len(groups))),
+            pltpu.SemaphoreType.DMA((4, 2)),
+            pltpu.SemaphoreType.DMA((t // tile,)),
         ],
         compiler_params=pltpu.CompilerParams(vmem_limit_bytes=VMEM_LIMIT, dimension_semantics=("arbitrary",)),
         cost_estimate=pl.CostEstimate(flops=6 * t * d * ff, bytes_accessed=6 * d * ff + 8 * t * d, transcendentals=t * ff),
@@ -230,8 +249,13 @@
                 for c in weights(block + 1):
                     c.start()
 
-            wgt[...] = wgb[slot].T
-            wut[...] = wub[slot].T
+        cut = -(-fs // 128) * 128
+        for which, at in ((0, slice(0, cut)), (1, slice(cut, f))):
+
+            @pl.when((half == which) & (tokens == 0))
+            def _(at=at):
+                wgt[at, :] = wgb[slot, :, at].T
+                wut[at, :] = wub[slot, :, at].T
 
         units_at = at_half(half)
         for i in range(TILES // 2):

time: 615 us -> 615 us (level)
  no operation moved by 1% of the time
where the time goes in v8:
time: 615 us
  Pallas kernels  601 us (98%)
  between operations  14.1 us (2%)
    pallas_call x1, Pallas kernels, backward(): pl.pallas_call(backward_kernel, out_shape=[jax.ShapeDtypeStruct((SUMMED,...  406 us
    pallas_call x2, Pallas kernels, adamw(): pl.pallas_call(functools.partial(adamw_kernel, tuple(rounds), first, len(...  141 us
    pallas_call x1, Pallas kernels, forward(): pl.pallas_call(functools.partial(forward_kernel, groups, shared), grid=(t...  53.5 us
  transfers between devices with their start and end apart: 1, of which 0 were waited for; matrix products, arithmetic and copies ran while one was open for 0% of the time, Pallas kernels for 20%

profile of v8, /device:TPU:27, one launch (start us, length us, event | category | flops | bytes accessed | tf_op | source)
XLA Modules:
  0.0 614.9 jit_solution(14952393661749957159)
XLA Ops:
  7.2 0.0 all-reduce.2.cloned.1.call-start
  7.2 53.5 %forward.1 = (bf16[2048,1024]{1,0:T(8,128)(2,1)}, bf16[2048,1024]{1,0:T(8,128)(2,1)}, bf16[2048,1024]{1,0:T(8,128)(2,1)}) custom-call(bf16[2048,1024]{1,0:T(8,128)(2,1)} %bitcast.2, bf16[2,1024,3200]{2,1,0:T(8,128)(2,1)} %refs_0_.3, bf16[2,1024,3200]{2,1,0:T(8,128)(2,1)} %refs_3_.3, bf16[2,3200,1024]{2,1,0:T(8,128)(2,1)} %refs_6_.3), custom_call_target="tpu_custom_call" | custom-call | flops 40265318400 | bytes 36438016 | tf_op jit(solution)/shard_map/forward/pallas_call | solution.py:108
  60.7 405.9 %backward.1 = (bf16[26,640,1024]{2,1,0:T(8,128)(2,1)}, bf16[4,640,1024]{2,1,0:T(8,128)(2,1)}, bf16[52,160,1024]{2,1,0:T(8,128)(2,1)}, bf16[52,160,1024]{2,1,0:T(8,128)(2,1)}) custom-call(bf16[2048,1024]{1,0:T(8,128)(2,1)} %get-tuple-element.32.a1_hbm, bf16[2048,1024]{1,0:T(8,128)(2,1)} %get-tuple-element.33.a0_hbm, ...), custom_call_target="tpu_custom_call" | custom-call | flops 201326592000 | bytes 327680000 | tf_op jit(solution)/shard_map/backward/pallas_call | solution.py:642
  466.6 0.0 all-reduce.2.cloned.1.call-update
  466.6 121.5 %adamw.2 = (bf16[2,1024,3200]{2,1,0:T(8,128)(2,1)}, f32[2,1024,3200]{2,1,0:T(8,128)}, f32[2,1024,3200]{2,1,0:T(8,128)}, bf16[2,1024,3200]{2,1,0:T(8,128)(2,1)}, ...) custom-call(bf16[2,1024,3200]{2,1,0:T(8,128)(2,1)} %refs_0_.3, ...), custom_call_target="tpu_custom_call" | custom-call | flops 34078720000 | bytes 374865920 | tf_op jit(solution)/shard_map/adamw/pallas_call | solution.py:827
  588.2 0.0 all-reduce.2.cloned.1.call-done.refs_9_
  588.2 19.9 %adamw.3 = (bf16[2,1024,3200]{2,1,0:T(8,128)(2,1)}, f32[2,1024,3200]{2,1,0:T(8,128)}, f32[2,1024,3200]{2,1,0:T(8,128)}, bf16[2,1024,3200]{2,1,0:T(8,128)(2,1)}, ...) custom-call(bf16[2,1024,3200]{2,1,0:T(8,128)(2,1)} %refs_0_.3, ...), custom_call_target="tpu_custom_call", output_to_operand_aliasing={{0}: (10, {}), {1}: (11, {}), {2}: (12, {}), {3}: (13, {}),... | custom-call | flops 5242880000 | bytes 57671680 | tf_op jit(solution)/shard_map/adamw/pallas_call | solution.py:827
Async XLA Ops:
  7.2 581.0 %all-reduce.2.cloned.1.call-start = ((), (), s32[]{:S(2)}) async-start(), calls=%async_computation | async-start | bytes 10485760 | tf_op jit(solution)/shard_map/psum | solution.py:864
Sparse Core Ops, SparseCore 0:
  466.8 115.5 all-reduce.1

commit v9 on v7

--- a/solution.py
+++ b/solution.py
@@ -6,7 +6,6 @@
 from jax.experimental import pallas as pl
 from jax.experimental.pallas import tpu as pltpu
 from jax.sharding import PartitionSpec as P
-
 
 BF16, F32 = jnp.bfloat16, jnp.float32
 MESH = pl.DeviceIdType.MESH
@@ -52,11 +51,8 @@
 
     @pl.when(first)
     def _():
-        for i in everything:
-            for c in loads(i)[:2]:
-                c.start()
-        for i in everything:
-            loads(i)[2].start()
+        for c in loads(0)[:2]:
+            c.start()
 
     wide = x_ref[...].astype(F32)
     a = (wide * scale_of(wide)).astype(BF16)
@@ -67,9 +63,15 @@
         def _(i=i):
             for c in loads(i)[:2]:
                 c.wait()
-            if i + 1 == len(groups):
+            if i + 1 < len(groups):
+                for c in loads(i + 1)[:2]:
+                    c.start()
+            if i + 2 >= len(groups):
                 for j in everything:
-                    loads(j)[2].wait()
+                    if i + 2 == len(groups) or len(groups) == 1:
+                        loads(j)[2].start()
+                    if i + 1 == len(groups):
+                        loads(j)[2].wait()
 
         for s, n in groups[i]:
             gate = dot(a, wg[:, s : s + n])
@@ -186,8 +188,6 @@
         a.start()
         if b is not None:
             b.start()
-    for c in load_tokens(1):
-        c.start()
     dat[...] = jnp.zeros_like(dat)
 
     barrier = pltpu.get_barrier_semaphore()
@@ -225,13 +225,23 @@
             for c in weights(block):
                 c.wait()
 
+            @pl.when(block == 0)
+            def _():
+                for c in load_tokens(1):
+                    c.start()
+
             @pl.when(block + 1 < 2 * BLOCKS)
             def _():
                 for c in weights(block + 1):
                     c.start()
 
-            wgt[...] = wgb[slot].T
-            wut[...] = wub[slot].T
+        cut = -(-fs // 128) * 128
+        for which, at in ((0, slice(0, cut)), (1, slice(cut, f))):
+
+            @pl.when((half == which) & (tokens == 0))
+            def _(at=at):
+                wgt[at, :] = wgb[slot, :, at].T
+                wut[at, :] = wub[slot, :, at].T
 
         units_at = at_half(half)
         for i in range(TILES // 2):

time: 615 us -> 613 us (level)
  no operation moved by 1% of the time
where the time goes in v9:
time: 613 us; the launch traced here: 612 us
  Pallas kernels  598 us (98%)
  between operations  14.1 us (2%)
    pallas_call x1, Pallas kernels, backward(): pl.pallas_call(backward_kernel, out_shape=[jax.ShapeDtypeStruct((SUMMED,...  406 us
    pallas_call x2, Pallas kernels, adamw(): pl.pallas_call(functools.partial(adamw_kernel, tuple(rounds), first, len(...  141 us
    pallas_call x1, Pallas kernels, forward(): pl.pallas_call(functools.partial(forward_kernel, groups), grid=(t // tile...  51.2 us
  transfers between devices with their start and end apart: 1, of which 0 were waited for; matrix products, arithmetic and copies ran while one was open for 0% of the time, Pallas kernels for 20%

profile of v9, /device:TPU:27, one launch (start us, length us, event | category | flops | bytes accessed | tf_op | source)
XLA Modules:
  0.0 612.3 jit_solution(7323994638229892242)
XLA Ops:
  7.2 0.0 all-reduce.2.cloned.1.call-start
  7.2 51.2 %forward.1 = (bf16[2048,1024]{1,0:T(8,128)(2,1)}, bf16[2048,1024]{1,0:T(8,128)(2,1)}, bf16[2048,1024]{1,0:T(8,128)(2,1)}) custom-call(bf16[2048,1024]{1,0:T(8,128)(2,1)} %bitcast.2, bf16[2,1024,3200]{2,1,0:T(8,128)(2,1)} %refs_0_.3, bf16[2,1024,3200]{2,1,0:T(8,128)(2,1)} %refs_3_.3, bf16[2,3200,1024]{2,1,0:T(8,128)(2,1)} %refs_6_.3), custom_call_target="tpu_custom_call" | custom-call | flops 40265318400 | bytes 36438016 | tf_op jit(solution)/shard_map/forward/pallas_call | solution.py:94
  58.4 405.5 %backward.1 = (bf16[26,640,1024]{2,1,0:T(8,128)(2,1)}, bf16[4,640,1024]{2,1,0:T(8,128)(2,1)}, bf16[52,160,1024]{2,1,0:T(8,128)(2,1)}, bf16[52,160,1024]{2,1,0:T(8,128)(2,1)}) custom-call(bf16[2048,1024]{1,0:T(8,128)(2,1)} %get-tuple-element.32.a1_hbm, bf16[2048,1024]{1,0:T(8,128)(2,1)} %get-tuple-element.33.a0_hbm, ...), custom_call_target="tpu_custom_call" | custom-call | flops 201326592000 | bytes 327680000 | tf_op jit(solution)/shard_map/backward/pallas_call | solution.py:628
  463.9 0.0 all-reduce.2.cloned.1.call-update
  464.0 121.5 %adamw.2 = (bf16[2,1024,3200]{2,1,0:T(8,128)(2,1)}, f32[2,1024,3200]{2,1,0:T(8,128)}, f32[2,1024,3200]{2,1,0:T(8,128)}, bf16[2,1024,3200]{2,1,0:T(8,128)(2,1)}, ...) custom-call(bf16[2,1024,3200]{2,1,0:T(8,128)(2,1)} %refs_0_.3, ...), custom_call_target="tpu_custom_call" | custom-call | flops 34078720000 | bytes 374865920 | tf_op jit(solution)/shard_map/adamw/pallas_call | solution.py:813
  585.5 0.0 all-reduce.2.cloned.1.call-done.refs_9_
  585.5 19.9 %adamw.3 = (bf16[2,1024,3200]{2,1,0:T(8,128)(2,1)}, f32[2,1024,3200]{2,1,0:T(8,128)}, f32[2,1024,3200]{2,1,0:T(8,128)}, bf16[2,1024,3200]{2,1,0:T(8,128)(2,1)}, ...) custom-call(bf16[2,1024,3200]{2,1,0:T(8,128)(2,1)} %refs_0_.3, ...), custom_call_target="tpu_custom_call", output_to_operand_aliasing={{0}: (10, {}), {1}: (11, {}), {2}: (12, {}), {3}: (13, {}),... | custom-call | flops 5242880000 | bytes 57671680 | tf_op jit(solution)/shard_map/adamw/pallas_call | solution.py:813
Async XLA Ops:
  7.2 578.3 %all-reduce.2.cloned.1.call-start = ((), (), s32[]{:S(2)}) async-start(), calls=%async_computation | async-start | bytes 10485760 | tf_op jit(solution)/shard_map/psum | solution.py:850
Sparse Core Ops, SparseCore 0:
  464.1 115.5 all-reduce.1
